TPU v7x, 256 devices: a 2x2x32 block of a 4x8x32 slice. The times are simulated.
256 devices in a mesh: groups: 4 (over x, y), gx: 64 (over z, core).
Axes of the slice: x: 2, y: 2, z: 32, core: 2. Of those that a mesh axis runs over, the one named last changes fastest.
The devices are a block of a 4x8x32 slice.
Arguments:
- positions: float32 [3, 1048576], P(None, ('groups', 'gx')), parts along dimension 1, may hold values from -0.08 to 127.08, as said below
- radii: float32 [1048576], P(('groups', 'gx')), parts along dimension 0, may hold values from 0.5 to 0.56
- neighbours: int32 [6, 1048576], P(None, ('groups', 'gx')), parts along dimension 1, may hold values from 0 to 262143, as said below
- right_side: float32 [3, 1048576], P(None, ('groups', 'gx')), parts along dimension 1, may hold values from -6 to 6
Outputs:
- solution_field: float32 [3, 1048576], P(None, ('groups', 'gx')), parts along dimension 1
- residual: float32 [3, 1048576], P(None, ('groups', 'gx')), parts along dimension 1
There are 4 independent parts, one for each index of `groups`. A program takes and returns all parts, laid end to end along the dimension named above; each array names one. Nothing has to cross between parts.
Inputs may be any that keep to these rules, and one draw needn't show every extreme that they name: `positions`: particles are ordered by lattice planes of 2048 along the first coordinate, rows of 128 within a plane; each lies within 0.08 of its lattice site in every coordinate. `neighbours`: each column lists distinct partners of the particle, the other slots hold the particle's own index; partnership is symmetric; every partner index is the particle's index plus or minus 1, 128 or 2048.
All inputs are finite; a program needn't handle non-finite values.
Results may differ from a plain program's by a relative error of at most 0.0003.
Values sent between devices are 32-bit elements; how exact they have to be, the bound alone decides.
No kernel may reach another device: no remote copies, remote signals or barrier semaphores. Data moves between devices by JAX's collectives and lax.ppermute only.
A program may use at most 64 MiB of HBM per device.

v0:
```python
import jax
import jax.numpy as jnp
from jax import lax
from jax.sharding import PartitionSpec as P

LY = 16
LZ = 128
ITERS = 4


diagonal_shift = 4.0


def sent_to_all(array, axis):
    copies = jnp.broadcast_to(array, (lax.axis_size(axis), *array.shape))
    return lax.all_to_all(copies, axis, split_axis=0, concat_axis=0, tiled=True)


def over_copies(array, axis):
    return sent_to_all(array, axis).sum(axis=0)


def together(arrays, axis):
    line, at, gathered = (jnp.concatenate([a.reshape(-1) for a in arrays]), 0, [])
    running = over_copies(line, axis)
    for a in arrays:
        gathered.append(running[at : at + a.size].reshape(a.shape))
        at += a.size
    return tuple(gathered)


def extended_2(array, sides, width):
    for axis, dim in sides:
        devices, length = (lax.axis_size(axis), array.shape[dim])
        up = [(i, (i + 1) % devices) for i in range(devices - 1)]
        down = [(j, i) for i, j in up]
        last = lax.slice_in_dim(array, length - width, length, axis=dim)
        first = lax.slice_in_dim(array, 0, width, axis=dim)
        before = lax.ppermute(last, axis, up)
        after = lax.ppermute(first, axis, down)
        array = jnp.concatenate([before, array, after], axis=dim)
    return array


def partner_values(extended, matches, offsets, owned, plane_size):
    own_view = extended[:, plane_size : plane_size + owned]
    partner = jnp.broadcast_to(
        own_view[:, None, :], (extended.shape[0], matches[0].shape[0], owned)
    )
    for which in range(len(offsets)):
        start = plane_size + offsets[which]
        view = extended[:, start : start + owned]
        partner = jnp.where(matches[which][None, :, :], view[:, None, :], partner)
    return partner


def pair_terms(own_geom, partner_geom, present):
    offset = partner_geom[:3] - own_geom[:3][:, None, :]
    squared = jnp.sum(offset * offset, axis=0)
    distance = jnp.sqrt(jnp.where(present, squared, jnp.float32(1.0)))
    normal = offset / distance
    contact = own_geom[3][None, :] + partner_geom[3]
    stiffness = 1.0 / (contact * contact)
    tension = -(1.0 - distance / contact) / (contact * distance)
    live_mask = present.astype(jnp.float32)
    return (normal, tension * live_mask, (stiffness - tension) * live_mask)


def apply_terms(vector, partner, blocks):
    normal, tension, radial = blocks
    relative = vector[:, None, :] - partner
    along_normal = jnp.sum(normal * relative, axis=0)
    return diagonal_shift * vector + jnp.sum(
        tension * relative + radial * normal * along_normal, axis=1
    )


def two_products(residual, image_vec):
    return together((jnp.sum(residual * residual), jnp.sum(residual * image_vec)), "gx")


def on_device(positions, radii, neighbours, right_side):
    owned = positions.shape[1]
    plane_size = LY * LZ
    first_id = lax.axis_index("gx") * owned
    own_ids = first_id + jnp.arange(owned, dtype=jnp.int32)
    present = neighbours != own_ids[None, :]
    offsets = [plane_size, -plane_size, LZ, -LZ, 1, -1]
    matches = [neighbours == (own_ids + shift_by)[None, :] for shift_by in offsets]
    geometry = jnp.concatenate([positions, radii[None, :]], axis=0)

    def operate(vector):
        joined = jnp.concatenate([geometry, vector], axis=0)
        extended = extended_2(joined, (("gx", 1),), plane_size)
        partner = partner_values(extended, matches, offsets, owned, plane_size)
        blocks = pair_terms(geometry, partner[:4], present)
        return apply_terms(vector, partner[4:], blocks)

    solution_field = jnp.zeros_like(right_side)
    residual = right_side
    image_vec = operate(residual)
    norm_now, product = two_products(residual, image_vec)
    step_size = norm_now / product
    direction = residual
    image_dir = image_vec
    for iteration in range(ITERS):
        solution_field = solution_field + step_size * direction
        residual = residual - step_size * image_dir
        if iteration + 1 < ITERS:
            image_vec = operate(residual)
            norm_next, product = two_products(residual, image_vec)
            beta_ratio = norm_next / norm_now
            step_size = norm_next / (product - beta_ratio * norm_next / step_size)
            direction = residual + beta_ratio * direction
            image_dir = image_vec + beta_ratio * image_dir
            norm_now = norm_next
    return (solution_field, residual)


def solution(mesh):
    return jax.shard_map(
        on_device,
        mesh=mesh,
        in_specs=(
            P(None, ("groups", "gx")),
            P(("groups", "gx")),
            P(None, ("groups", "gx")),
            P(None, ("groups", "gx")),
        ),
        out_specs=(P(None, ("groups", "gx")), P(None, ("groups", "gx"))),
        check_vma=False,
    )
```

profile of v0, /device:TPU:37, one launch (start us, length us, event | category | flops | bytes accessed | tf_op | source)
XLA Modules:
  0.0 209.7 jit_solution(9159718237776236838)
XLA Ops:
  0.6 0.9 pad_maximum_fusion.3
  1.6 5.2 %collective-permute-start = (f32[7,2048]{1,0:T(8,128)S(1)}, f32[7,2048]{1,0:T(8,128)S(1)}, u32[]{:S(2)}, u32[]{:S(2)}) collective-permute-start(f32[7,2048]{1,0:T(8,128)S(1)} %get-tuple-element.71), channel_id=1, source_target_pairs={{0,1},{1,2},{2,3},{3,4},{4,5},{5,6},{6,7},{7,8},{8,9},{9,10},{10,1... | collective-permute-start | bytes 172040 | tf_op jit(solution)/shard_map/ppermute | solution.py:39
  6.8 18.6 %collective-permute-start.1 = (f32[7,2048]{1,0:T(8,128)S(1)}, f32[7,2048]{1,0:T(8,128)S(1)}, u32[]{:S(2)}, u32[]{:S(2)}) collective-permute-start(f32[7,2048]{1,0:T(8,128)S(1)} %get-tuple-element.72), channel_id=1, source_target_pairs={{1,0},{2,1},{3,2},{4,3},{5,4},{6,5},{7,6},{8,7},{9,8},{10,9},{11,1... | collective-permute-start | bytes 172040 | tf_op jit(solution)/shard_map/ppermute | solution.py:40
  28.2 1.4 pad_maximum_fusion.5
  29.6 40.5 %all_to_all.24 = f32[64,1,2]{2,1,0:T(1,128)S(1)} all-to-all(f32[64,1,2]{2,1,0:T(1,128)S(1)} %broadcast_in_dim.347), channel_id=1, replica_groups=mesh['groups'=4,'gx'=64] {'gx'}, dimensions={0} | all-to-all | bytes 1024 | tf_op jit(solution)/shard_map/all_to_all | solution.py:16
  72.2 3.6 %collective-permute-start.2 = (f32[7,2048]{1,0:T(8,128)S(1)}, f32[7,2048]{1,0:T(8,128)S(1)}, u32[]{:S(2)}, u32[]{:S(2)}) collective-permute-start(f32[7,2048]{1,0:T(8,128)S(1)} %get-tuple-element.63), channel_id=1, source_target_pairs={{0,1},{1,2},{2,3},{3,4},{4,5},{5,6},{6,7},{7,8},{8,9},{9,10},{10,1... | collective-permute-start | bytes 172040 | tf_op jit(solution)/shard_map/ppermute | solution.py:39
  75.8 2.0 collective-permute-start.3
  77.8 3.6 %collective-permute-done.3 = f32[7,2048]{1,0:T(8,128)S(1)} collective-permute-done((f32[7,2048]{1,0:T(8,128)S(1)}, f32[7,2048]{1,0:T(8,128)S(1)}, u32[]{:S(2)}, u32[]{:S(2)}) %collective-permute-start.3) | collective-permute-done | bytes 57376 | tf_op jit(solution)/shard_map/ppermute | solution.py:40
  82.6 0.7 multiply_reduce_fusion.13
  83.4 1.3 pad_maximum_fusion.6
  84.7 28.2 %all_to_all.25 = f32[64,1,2]{2,1,0:T(1,128)S(1)} all-to-all(f32[64,1,2]{2,1,0:T(1,128)S(1)} %broadcast_in_dim.355), channel_id=1, replica_groups=mesh['groups'=4,'gx'=64] {'gx'}, dimensions={0} | all-to-all | bytes 1024 | tf_op jit(solution)/shard_map/all_to_all | solution.py:16
  113.0 0.7 fusion.43
  118.2 3.6 %collective-permute-start.4 = (f32[7,2048]{1,0:T(8,128)S(1)}, f32[7,2048]{1,0:T(8,128)S(1)}, u32[]{:S(2)}, u32[]{:S(2)}) collective-permute-start(f32[7,2048]{1,0:T(8,128)S(1)} %get-tuple-element.61), channel_id=1, source_target_pairs={{0,1},{1,2},{2,3},{3,4},{4,5},{5,6},{6,7},{7,8},{8,9},{9,10},{10,1... | collective-permute-start | bytes 172040 | tf_op jit(solution)/shard_map/ppermute | solution.py:39
  121.8 2.0 collective-permute-start.5
  123.8 3.6 %collective-permute-done.5 = f32[7,2048]{1,0:T(8,128)S(1)} collective-permute-done((f32[7,2048]{1,0:T(8,128)S(1)}, f32[7,2048]{1,0:T(8,128)S(1)}, u32[]{:S(2)}, u32[]{:S(2)}) %collective-permute-start.5) | collective-permute-done | bytes 57376 | tf_op jit(solution)/shard_map/ppermute | solution.py:40
  129.2 1.4 pad_maximum_fusion.7
  130.6 28.2 %all_to_all.26 = f32[64,1,2]{2,1,0:T(1,128)S(1)} all-to-all(f32[64,1,2]{2,1,0:T(1,128)S(1)} %broadcast_in_dim.363), channel_id=1, replica_groups=mesh['groups'=4,'gx'=64] {'gx'}, dimensions={0} | all-to-all | bytes 1024 | tf_op jit(solution)/shard_map/all_to_all | solution.py:16
  163.4 3.6 %collective-permute-start.6 = (f32[7,2048]{1,0:T(8,128)S(1)}, f32[7,2048]{1,0:T(8,128)S(1)}, u32[]{:S(2)}, u32[]{:S(2)}) collective-permute-start(f32[7,2048]{1,0:T(8,128)S(1)} %get-tuple-element.59), channel_id=1, source_target_pairs={{0,1},{1,2},{2,3},{3,4},{4,5},{5,6},{6,7},{7,8},{8,9},{9,10},{10,1... | collective-permute-start | bytes 172040 | tf_op jit(solution)/shard_map/ppermute | solution.py:39
  167.0 2.0 collective-permute-start.7
  169.0 3.6 %collective-permute-done.7 = f32[7,2048]{1,0:T(8,128)S(1)} collective-permute-done((f32[7,2048]{1,0:T(8,128)S(1)}, f32[7,2048]{1,0:T(8,128)S(1)}, u32[]{:S(2)}, u32[]{:S(2)}) %collective-permute-start.7) | collective-permute-done | bytes 57376 | tf_op jit(solution)/shard_map/ppermute | solution.py:40
  173.8 0.7 multiply_reduce_fusion.9
  174.5 1.4 pad_maximum_fusion.8
  176.0 28.2 %all_to_all.27 = f32[64,1,2]{2,1,0:T(1,128)S(1)} all-to-all(f32[64,1,2]{2,1,0:T(1,128)S(1)} %broadcast_in_dim.371), channel_id=1, replica_groups=mesh['groups'=4,'gx'=64] {'gx'}, dimensions={0} | all-to-all | bytes 1024 | tf_op jit(solution)/shard_map/all_to_all | solution.py:16
  209.0 0.8 multiply_subtract_fusion
  (73 shorter events, 9.3 us)
Async XLA Ops:
  1.6 23.9 %copy-start.3 = (s32[6,4096]{1,0:T(8,128)S(1)}, s32[6,4096]{1,0:T(8,128)}, u32[]{:S(2)}) copy-start(s32[6,4096]{1,0:T(8,128)} %param.6) | copy-start | bytes 294916
  1.6 24.0 %collective-permute-start = (f32[7,2048]{1,0:T(8,128)S(1)}, f32[7,2048]{1,0:T(8,128)S(1)}, u32[]{:S(2)}, u32[]{:S(2)}) collective-permute-start(f32[7,2048]{1,0:T(8,128)S(1)} %get-tuple-element.71), channel_id=1, source_target_pairs={{0,1},{1,2},{2,3},{3,4},{4,5},{5,6},{6,7},{7,8},{8,9},{9,10},{10,1... | collective-permute-start | bytes 172040 | tf_op jit(solution)/shard_map/ppermute | solution.py:39
  6.8 19.5 %collective-permute-start.1 = (f32[7,2048]{1,0:T(8,128)S(1)}, f32[7,2048]{1,0:T(8,128)S(1)}, u32[]{:S(2)}, u32[]{:S(2)}) collective-permute-start(f32[7,2048]{1,0:T(8,128)S(1)} %get-tuple-element.72), channel_id=1, source_target_pairs={{1,0},{2,1},{3,2},{4,3},{5,4},{6,5},{7,6},{8,7},{9,8},{10,9},{11,1... | collective-permute-start | bytes 172040 | tf_op jit(solution)/shard_map/ppermute | solution.py:40
  25.5 0.8 copy-start
  25.5 0.9 copy-start.1
  25.5 0.9 copy-start.2
  72.2 5.6 %collective-permute-start.2 = (f32[7,2048]{1,0:T(8,128)S(1)}, f32[7,2048]{1,0:T(8,128)S(1)}, u32[]{:S(2)}, u32[]{:S(2)}) collective-permute-start(f32[7,2048]{1,0:T(8,128)S(1)} %get-tuple-element.63), channel_id=1, source_target_pairs={{0,1},{1,2},{2,3},{3,4},{4,5},{5,6},{6,7},{7,8},{8,9},{9,10},{10,1... | collective-permute-start | bytes 172040 | tf_op jit(solution)/shard_map/ppermute | solution.py:39
  75.8 5.6 %collective-permute-start.3 = (f32[7,2048]{1,0:T(8,128)S(1)}, f32[7,2048]{1,0:T(8,128)S(1)}, u32[]{:S(2)}, u32[]{:S(2)}) collective-permute-start(f32[7,2048]{1,0:T(8,128)S(1)} %get-tuple-element.64), channel_id=1, source_target_pairs={{1,0},{2,1},{3,2},{4,3},{5,4},{6,5},{7,6},{8,7},{9,8},{10,9},{11,1... | collective-permute-start | bytes 172040 | tf_op jit(solution)/shard_map/ppermute | solution.py:40
  118.2 5.6 %collective-permute-start.4 = (f32[7,2048]{1,0:T(8,128)S(1)}, f32[7,2048]{1,0:T(8,128)S(1)}, u32[]{:S(2)}, u32[]{:S(2)}) collective-permute-start(f32[7,2048]{1,0:T(8,128)S(1)} %get-tuple-element.61), channel_id=1, source_target_pairs={{0,1},{1,2},{2,3},{3,4},{4,5},{5,6},{6,7},{7,8},{8,9},{9,10},{10,1... | collective-permute-start | bytes 172040 | tf_op jit(solution)/shard_map/ppermute | solution.py:39
  121.8 5.6 %collective-permute-start.5 = (f32[7,2048]{1,0:T(8,128)S(1)}, f32[7,2048]{1,0:T(8,128)S(1)}, u32[]{:S(2)}, u32[]{:S(2)}) collective-permute-start(f32[7,2048]{1,0:T(8,128)S(1)} %get-tuple-element.62), channel_id=1, source_target_pairs={{1,0},{2,1},{3,2},{4,3},{5,4},{6,5},{7,6},{8,7},{9,8},{10,9},{11,1... | collective-permute-start | bytes 172040 | tf_op jit(solution)/shard_map/ppermute | solution.py:40
  163.4 5.6 %collective-permute-start.6 = (f32[7,2048]{1,0:T(8,128)S(1)}, f32[7,2048]{1,0:T(8,128)S(1)}, u32[]{:S(2)}, u32[]{:S(2)}) collective-permute-start(f32[7,2048]{1,0:T(8,128)S(1)} %get-tuple-element.59), channel_id=1, source_target_pairs={{0,1},{1,2},{2,3},{3,4},{4,5},{5,6},{6,7},{7,8},{8,9},{9,10},{10,1... | collective-permute-start | bytes 172040 | tf_op jit(solution)/shard_map/ppermute | solution.py:39
  167.0 5.6 %collective-permute-start.7 = (f32[7,2048]{1,0:T(8,128)S(1)}, f32[7,2048]{1,0:T(8,128)S(1)}, u32[]{:S(2)}, u32[]{:S(2)}) collective-permute-start(f32[7,2048]{1,0:T(8,128)S(1)} %get-tuple-element.60), channel_id=1, source_target_pairs={{1,0},{2,1},{3,2},{4,3},{5,4},{6,5},{7,6},{8,7},{9,8},{10,9},{11,1... | collective-permute-start | bytes 172040 | tf_op jit(solution)/shard_map/ppermute | solution.py:40
where the time goes:
time: 211 us; the launch traced here: 210 us
  blocking collectives  125 us (59%)
  starting transfers between devices  40.5 us (19%)
  between operations  14.7 us (7%)
  other arithmetic  14.5 us (7%)
  waiting for transfers between devices  11.6 us (5%)
  local copies, waits for them, and re-layouts  3.37 us (2%)
    all_to_all x4, blocking collectives, sent_to_all(): return lax.all_to_all(copies, axis, split_axis=0, concat_axis=0, tiled=True)  125 us
    ppermute x4, starting transfers between devices, extended_2(): after = lax.ppermute(first, axis, down)  24.4 us
    ppermute x4, starting transfers between devices, extended_2(): before = lax.ppermute(last, axis, up)  16.1 us
    ppermute x4, waiting for transfers between devices, extended_2(): after = lax.ppermute(first, axis, down)  11.6 us
    concatenate x4, other arithmetic, together(): jnp.concatenate([a.reshape(-1) for a in arrays])  5.46 us
  transfers between devices with their start and end apart: 8, of which 4 were waited for; matrix products, arithmetic and copies ran while one was open for 0% of the time, Pallas kernels for 0%

commit v1 on v0

v1 whole, which is shorter than its diff:
```python
import jax
import jax.numpy as jnp
from jax import lax
from jax.experimental import pallas as pl
from jax.experimental.pallas import tpu as pltpu
from jax.sharding import PartitionSpec as P

LY = 16
LZ = 128
ITERS = 4
DIAGONAL_SHIFT = 4.0

CENTER = 5.7
RADIUS = 2.3
ORIGIN = -CENTER / RADIUS
MOMENTS = 2 * ITERS
LOWEST, HIGHEST = -2.2, 4.6

f32 = jnp.float32


def second_kind(order):
    below, value = 0.0, 1.0
    for _ in range(order):
        below, value = value, 2.0 * ORIGIN * value - below
    return value


def pack_kernel(first_ref, pos_ref, rad_ref, nb_ref, rhs_ref, out_ref):
    rows = rad_ref.shape[0]
    shape = (rows, LZ)
    ids = first_ref[0] + (
        lax.broadcasted_iota(jnp.int32, shape, 0) * LZ
        + lax.broadcasted_iota(jnp.int32, shape, 1)
    )
    for c in range(3):
        out_ref[c] = pos_ref[:, c, :]
        out_ref[7 + c] = rhs_ref[:, c, :]
    out_ref[3] = rad_ref[...]
    slots = [nb_ref[:, s, :] - ids for s in range(nb_ref.shape[1])]
    for b, shift in enumerate((LY * LZ, LZ, 1)):
        hit = slots[0] == shift
        for other in slots[1:]:
            hit = hit | (other == shift)
        out_ref[4 + b] = jnp.where(hit, f32(1.0), f32(0.0))


def up_row(x):
    return pltpu.roll(x, x.shape[0] - 1, 0)


def down_row(x):
    return pltpu.roll(x, 1, 0)


def next_lane(x, x_up, lane):
    return pltpu.roll(jnp.where(lane == 0, x_up, x), LZ - 1, 1)


def bond(mask, delta, contact):
    squared = delta[0] * delta[0] + delta[1] * delta[1] + delta[2] * delta[2]
    live = mask > 0.5
    squared = jnp.where(live, squared, f32(1.0))
    inverse = 1.0 / (contact * jnp.sqrt(squared))
    tension = (squared * inverse - 1.0) * inverse
    over = inverse * contact
    weight = jnp.sqrt(inverse) * over
    tension = jnp.where(live, tension, f32(0.0))
    weight = jnp.where(live, weight, f32(0.0))
    return tension, [d * weight for d in delta]


def flux(pair, here, there):
    tension, w = pair
    rel = [a - b for a, b in zip(here, there)]
    along = w[0] * rel[0] + w[1] * rel[1] + w[2] * rel[2]
    return [tension * r + along * n for r, n in zip(rel, w)]


def cut(values, lo, hi):
    return [v[lo:hi] for v in values]


def krylov_kernel(ll_ref, l_ref, own_ref, r_ref, rr_ref, basis_ref, sums_ref):
    rows = own_ref.shape[1]
    depth = 2 * rows
    total = rows + 2 * depth

    def ext(c):
        return jnp.concatenate(
            [ref[c] for ref in (ll_ref, l_ref, own_ref, r_ref, rr_ref)], axis=0
        )

    lane = lax.broadcasted_iota(jnp.int32, (total, LZ), 1)
    geom = [ext(c) for c in range(4)]
    masks = [ext(4 + c) for c in range(3)]
    vector = [ext(7 + c) for c in range(3)]

    ahead = [g[LY:] for g in geom]
    base = [g[: total - LY] for g in geom]
    bond_x = bond(
        masks[0][: total - LY],
        [a - b for a, b in zip(ahead[:3], base[:3])],
        ahead[3] + base[3],
    )
    ups = [up_row(g) for g in geom]
    bond_y = bond(masks[1], [a - b for a, b in zip(ups[:3], geom[:3])], ups[3] + geom[3])
    nexts = [next_lane(g, u, lane) for g, u in zip(geom, ups)]
    bond_z = bond(
        masks[2], [a - b for a, b in zip(nexts[:3], geom[:3])], nexts[3] + geom[3]
    )

    def pair_at(pair, lo, hi):
        return pair[0][lo:hi], cut(pair[1], lo, hi)

    def operate(v, lo, hi):
        n = hi - lo
        here = cut(v, 0, n - LY)
        fx = flux(pair_at(bond_x, lo, hi - LY), here, cut(v, LY, n))
        a, b = lo + 8, hi - 8
        mid = cut(v, 8, n - 8)
        up = [x[8 : n - 8] for x in (up_row(x) for x in v)]
        ln = lane[: b - a]
        fy = flux(pair_at(bond_y, a, b), mid, up)
        nxt = [next_lane(x, u, ln) for x, u in zip(mid, up)]
        fz = flux(pair_at(bond_z, a, b), mid, nxt)
        result = []
        m = n - 2 * LY
        for c in range(3):
            rolled = pltpu.roll(fz[c], 1, 1)
            first = ln == 0
            back = down_row(fy[c] + jnp.where(first, rolled, f32(0.0)))
            side = fy[c] + fz[c] - back - jnp.where(first, f32(0.0), rolled)
            straight = fx[c][LY : LY + m] - fx[c][:m]
            result.append(
                f32(DIAGONAL_SHIFT - CENTER) * v[c][LY : LY + m]
                + straight
                + side[8 : 8 + m]
            )
        return result

    own = slice(depth, depth + rows)
    kept = [[x[own] for x in vector]]
    lo, hi = 0, total
    before, now = None, vector
    for k in range(ITERS):
        image = operate(now, lo, hi)
        m = hi - lo - 2 * LY
        if k == 0:
            after = [x * f32(1.0 / RADIUS) for x in image]
        else:
            after = [
                x * f32(2.0 / RADIUS) - p[2 * LY : 2 * LY + m]
                for x, p in zip(image, before)
            ]
        before, now = now, after
        lo, hi = lo + LY, hi - LY
        kept.append([x[depth - lo : depth - lo + rows] for x in now])
    for k in range(ITERS + 1):
        for c in range(3):
            basis_ref[3 * k + c] = kept[k][c]

    sub = lax.broadcasted_iota(jnp.int32, (8, LZ), 0)
    col = lax.broadcasted_iota(jnp.int32, (8, LZ), 1)
    line = jnp.zeros((8, LZ), f32)
    for k in range(MOMENTS):
        i = k // 2
        j = k - i
        prod = (
            kept[i][0] * kept[j][0] + kept[i][1] * kept[j][1] + kept[i][2] * kept[j][2]
        )
        part = prod[:8]
        for r in range(8, rows, 8):
            part = part + prod[r : r + 8]
        for s in (4, 2, 1):
            part = part + pltpu.roll(part, s, 0)
        line = jnp.where(sub == k, part, line)
    for s in (64, 32, 16):
        line = line + pltpu.roll(line, s, 1)
    line = jnp.where(col // 16 == sub, line, f32(0.0))
    for s in (4, 2, 1):
        line = line + pltpu.roll(line, s, 0)
    sums_ref[...] = jnp.broadcast_to(line[:1][None], sums_ref.shape)


def coefficients(products):
    m = list(products[:2])
    for k in range(2, MOMENTS):
        m.append(2.0 * products[k] - m[k % 2])
    zero = jnp.zeros_like(m[0])
    one = jnp.ones_like(m[0])
    s_before, s = [zero] * MOMENTS, m
    alpha, beta = s[1] / s[0], None
    ratio = alpha
    c_before, c = [zero] * (ITERS + 1), [one] + [zero] * ITERS
    p_before, p = zero, one
    floor = s[0] * f32(1e-12)
    for k in range(ITERS):
        alpha = jnp.clip(alpha, LOWEST, HIGHEST)
        nc = [zero] * (ITERS + 1)
        for l in range(k + 1):
            if l == 0:
                nc[1] = nc[1] + c[0]
            else:
                nc[l - 1] = nc[l - 1] + 0.5 * c[l]
                nc[l + 1] = nc[l + 1] + 0.5 * c[l]
        for l in range(k + 1):
            nc[l] = nc[l] - alpha * c[l]
            if beta is not None and l < k:
                nc[l] = nc[l] - beta * c_before[l]
        np_ = (ORIGIN - alpha) * p
        if beta is not None:
            np_ = np_ - beta * p_before
        if k + 1 < ITERS:
            ns = [zero] * MOMENTS
            for l in range(k + 1, MOMENTS - k - 1):
                ns[l] = 0.5 * (s[l + 1] + s[abs(l - 1)]) - alpha * s[l]
                if beta is not None:
                    ns[l] = ns[l] - beta * s_before[l]
            q = k + 1
            den = jnp.maximum(ns[q], floor)
            factor = 1.0 if q == 1 else 0.5
            next_beta = factor * den / jnp.maximum(s[q - 1], floor)
            new_ratio = ns[q + 1] / den * 0.5
            alpha = new_ratio - ratio
            ratio = new_ratio
            s_before, s = s, ns
            beta = next_beta
        c_before, c = c, nc
        p_before, p = p, np_
    scale = 1.0 / p
    res = [x * scale for x in c]
    sol = []
    for i in range(ITERS):
        total = zero
        for j in range(i + 1, ITERS + 1):
            total = total + res[j] * f32(second_kind(j - 1 - i))
        sol.append(total * f32((-1.0 if i == 0 else -2.0) / RADIUS))
    return res, sol


def finish_kernel(basis_ref, sums_ref, sol_ref, res_ref):
    line = jnp.sum(sums_ref[...], axis=0)
    line = jnp.sum(line, axis=0, keepdims=True)
    line = jnp.broadcast_to(line, (8, LZ))
    for s in (8, 4, 2, 1):
        line = line + pltpu.roll(line, s, 1)
    products = [
        jnp.broadcast_to(line[:, 16 * k + 15 : 16 * k + 16], (8, LZ))
        for k in range(MOMENTS)
    ]
    res, sol = coefficients(products)
    rows = basis_ref.shape[1]
    for c in range(3):
        for r in range(0, rows, 8):
            t = [basis_ref[3 * k + c, r : r + 8, :] for k in range(ITERS + 1)]
            x = sol[0] * t[0]
            for k in range(1, ITERS):
                x = x + sol[k] * t[k]
            y = res[0] * t[0]
            for k in range(1, ITERS + 1):
                y = y + res[k] * t[k]
            sol_ref[r : r + 8, c, :] = x
            res_ref[r : r + 8, c, :] = y


def by_rows(array):
    return array.reshape(array.shape[0], -1, LZ).transpose(1, 0, 2)


def on_device(positions, radii, neighbours, right_side):
    owned = positions.shape[1]
    rows = owned // LZ
    devices = lax.axis_size("gx")
    first = (lax.axis_index("gx") * owned).astype(jnp.int32).reshape(1)
    vmem = pl.BlockSpec(memory_space=pltpu.VMEM)
    smem = pl.BlockSpec(memory_space=pltpu.SMEM)

    packed = pl.pallas_call(
        pack_kernel,
        out_shape=jax.ShapeDtypeStruct((10, rows, LZ), f32),
        in_specs=[smem, vmem, vmem, vmem, vmem],
        out_specs=vmem,
        compiler_params=pltpu.CompilerParams(vmem_limit_bytes=4 << 20),
        name="pack",
    )(
        first,
        by_rows(positions),
        radii.reshape(rows, LZ),
        by_rows(neighbours),
        by_rows(right_side),
    )

    def moved(array, by):
        pairs = [(i, (i + by) % devices) for i in range(devices)]
        return lax.ppermute(array, "gx", pairs)

    left, right = moved(packed, 1), moved(packed, -1)
    far_left, far_right = moved(packed, 2), moved(packed, -2)

    basis, sums = pl.pallas_call(
        krylov_kernel,
        out_shape=(
            jax.ShapeDtypeStruct((3 * (ITERS + 1), rows, LZ), f32),
            jax.ShapeDtypeStruct((devices, 1, LZ), f32),
        ),
        in_specs=[vmem] * 5,
        out_specs=(vmem, vmem),
        compiler_params=pltpu.CompilerParams(vmem_limit_bytes=12 << 20),
        name="krylov",
    )(far_left, left, packed, right, far_right)

    everyone = lax.all_to_all(sums, "gx", split_axis=0, concat_axis=0, tiled=True)

    sol, res = pl.pallas_call(
        finish_kernel,
        out_shape=(
            jax.ShapeDtypeStruct((rows, 3, LZ), f32),
            jax.ShapeDtypeStruct((rows, 3, LZ), f32),
        ),
        in_specs=[vmem, vmem],
        out_specs=(vmem, vmem),
        compiler_params=pltpu.CompilerParams(vmem_limit_bytes=4 << 20),
        name="finish",
    )(basis, everyone.reshape(-1, 8, LZ))
    back = lambda a: a.transpose(1, 0, 2).reshape(3, owned)
    return back(sol), back(res)


def solution(mesh):
    return jax.shard_map(
        on_device,
        mesh=mesh,
        in_specs=(
            P(None, ("groups", "gx")),
            P(("groups", "gx")),
            P(None, ("groups", "gx")),
            P(None, ("groups", "gx")),
        ),
        out_specs=(P(None, ("groups", "gx")), P(None, ("groups", "gx"))),
        check_vma=False,
    )
```

time: 211 us -> 72 us (0.34)
  blocking collectives: 125 us -> 31.8 us
  starting transfers between devices: 40.5 us -> 25.4 us
  other arithmetic: 14.5 us -> 0 us
  between operations: 14.7 us -> 0.66 us
  waiting for transfers between devices: 11.6 us -> 7.95 us
  Pallas kernels: 0 us -> 2.51 us
    all_to_all x4 -> x1, blocking collectives: 125 us -> 31.8 us  [on_device(): lax.all_to_all(sums, 'gx', split_axis=0, concat_axis=0, tiled=True)]
    ppermute x8 -> x4, starting transfers between devices: 40.5 us -> 25.4 us  [moved(): return lax.ppermute(array, 'gx', pairs)]
    concatenate x12 -> x0, other arithmetic: 6.77 us -> none  [the longest x4 5.46 us: together(): jnp.concatenate([a.reshape(-1) for a in arrays])]
    reduce_sum x20 -> x0, other arithmetic: 4.85 us -> none  [the longest x4 2.72 us: two_products(): jnp.sum(residual * residual)]
    ppermute x8 -> x4, waiting for transfers between devices: 11.6 us -> 7.95 us  [moved(): return lax.ppermute(array, 'gx', pairs)]
    unnamed x8, local copies, waits for them, and re-layouts: 0.09 us -> 3.29 us
    slice x15 -> x0, local copies, waits for them, and re-layouts: 3.19 us -> none  [the longest x4 2.43 us: together(): gathered.append(running[at:at + a.size].reshape(a.shape))]
    pallas_call x0 -> x3, Pallas kernels: none -> 2.51 us  [the longest x1 1.23 us: on_device(): pl.pallas_call(krylov_kernel, out_shape=(jax.ShapeDtypeStruct((3 * (ITERS...]
  transfers between devices with their start and end apart: 8 -> 4, of which waited for: 4 -> 4; matrix products, arithmetic and copies ran while one was open for 0% -> 0% of each run, Pallas kernels for 0% -> 0%
where the time goes in v1:
time: 72 us; the launch traced here: 71.6 us
  blocking collectives  31.8 us (44%)
  starting transfers between devices  25.4 us (35%)
  waiting for transfers between devices  7.95 us (11%)
  local copies, waits for them, and re-layouts  3.29 us (5%)
  Pallas kernels  2.51 us (3%)
    all_to_all x1, blocking collectives, on_device(): lax.all_to_all(sums, 'gx', split_axis=0, concat_axis=0, tiled=True)  31.8 us
    ppermute x4, starting transfers between devices, moved(): return lax.ppermute(array, 'gx', pairs)  25.4 us
    ppermute x4, waiting for transfers between devices, moved(): return lax.ppermute(array, 'gx', pairs)  7.95 us
    unnamed x8, local copies, waits for them, and re-layouts  3.29 us
  transfers between devices with their start and end apart: 4, of which 4 were waited for; matrix products, arithmetic and copies ran while one was open for 0% of the time, Pallas kernels for 0%

profile of v1, /device:TPU:37, one launch (start us, length us, event | category | flops | bytes accessed | tf_op | source)
XLA Modules:
  0.0 71.6 jit_solution(1972516381988016389)
XLA Ops:
  0.6 0.0 copy-start.3
  0.6 0.7 copy-done.3
  1.3 0.0 copy-start
  1.4 0.9 %copy-done = s32[6,4096]{1,0:T(8,128)S(1)} copy-done((s32[6,4096]{1,0:T(8,128)S(1)}, s32[6,4096]{1,0:T(8,128)}, u32[]{:S(2)}) %copy-start) | copy-done | bytes 98328
  2.3 0.0 copy-start.1
  2.3 0.8 %copy-done.1 = f32[3,4096]{1,0:T(4,128)S(1)} copy-done((f32[3,4096]{1,0:T(4,128)S(1)}, f32[3,4096]{1,0:T(4,128)}, u32[]{:S(2)}) %copy-start.1) | copy-done | bytes 49176
  3.1 0.0 copy-start.2
  3.1 0.8 %copy-done.2 = f32[3,4096]{1,0:T(4,128)S(1)} copy-done((f32[3,4096]{1,0:T(4,128)S(1)}, f32[3,4096]{1,0:T(4,128)}, u32[]{:S(2)}) %copy-start.2) | copy-done | bytes 49176
  3.9 0.1 pack.1.own_ref
  4.1 23.7 %collective-permute-start.3 = (f32[10,32,128]{2,1,0:T(8,128)S(1)}, f32[10,32,128]{2,1,0:T(8,128)S(1)}, u32[]{:S(2)}, u32[]{:S(2)}) collective-permute-start(f32[10,32,128]{2,1,0:T(8,128)S(1)} %pack.1.own_ref), channel_id=1, source_target_pairs={{0,62},{1,63},{2,0},{3,1},{4,2},{5,3},{6,4},{7,5},{8,6},{9,7},{10,... | collective-permute-start | bytes 491528 | tf_op jit(solution)/shard_map/ppermute | solution.py:296
  27.8 0.9 %collective-permute-start.2 = (f32[10,32,128]{2,1,0:T(8,128)S(1)}, f32[10,32,128]{2,1,0:T(8,128)S(1)}, u32[]{:S(2)}, u32[]{:S(2)}) collective-permute-start(f32[10,32,128]{2,1,0:T(8,128)S(1)} %pack.1.own_ref), channel_id=1, source_target_pairs={{0,63},{1,0},{2,1},{3,2},{4,3},{5,4},{6,5},{7,6},{8,7},{9,8},{10,9... | collective-permute-start | bytes 491528 | tf_op jit(solution)/shard_map/ppermute | solution.py:296
  28.6 0.9 %collective-permute-start.1 = (f32[10,32,128]{2,1,0:T(8,128)S(1)}, f32[10,32,128]{2,1,0:T(8,128)S(1)}, u32[]{:S(2)}, u32[]{:S(2)}) collective-permute-start(f32[10,32,128]{2,1,0:T(8,128)S(1)} %pack.1.own_ref), channel_id=1, source_target_pairs={{0,1},{1,2},{2,3},{3,4},{4,5},{5,6},{6,7},{7,8},{8,9},{9,10},{10,1... | collective-permute-start | bytes 491528 | tf_op jit(solution)/shard_map/ppermute | solution.py:296
  29.5 0.0 collective-permute-start
  29.5 1.2 %collective-permute-done.3.rr_ref = f32[10,32,128]{2,1,0:T(8,128)S(1)} collective-permute-done((f32[10,32,128]{2,1,0:T(8,128)S(1)}, f32[10,32,128]{2,1,0:T(8,128)S(1)}, u32[]{:S(2)}, u32[]{:S(2)}) %collective-permute-start.3) | collective-permute-done | bytes 163872 | tf_op jit(solution)/shard_map/ppermute | solution.py:296
  30.7 2.1 %collective-permute-done.2.r_ref = f32[10,32,128]{2,1,0:T(8,128)S(1)} collective-permute-done((f32[10,32,128]{2,1,0:T(8,128)S(1)}, f32[10,32,128]{2,1,0:T(8,128)S(1)}, u32[]{:S(2)}, u32[]{:S(2)}) %collective-permute-start.2) | collective-permute-done | bytes 163872 | tf_op jit(solution)/shard_map/ppermute | solution.py:296
  32.8 0.1 collective-permute-done.1.l_ref
  32.9 4.5 %collective-permute-done.ll_ref = f32[10,32,128]{2,1,0:T(8,128)S(1)} collective-permute-done((f32[10,32,128]{2,1,0:T(8,128)S(1)}, f32[10,32,128]{2,1,0:T(8,128)S(1)}, u32[]{:S(2)}, u32[]{:S(2)}) %collective-permute-start) | collective-permute-done | bytes 163872 | tf_op jit(solution)/shard_map/ppermute | solution.py:296
  37.5 1.2 %krylov.1 = (f32[15,32,128]{2,1,0:T(8,128)S(1)}, f32[64,1,128]{2,1,0:T(1,128)S(1)}) custom-call(f32[10,32,128]{2,1,0:T(8,128)S(1)} %collective-permute-done.ll_ref, f32[10,32,128]{2,1,0:T(8,128)S(1)} %collective-permute-done.1.l_ref, f32[10,32,128]{2,1,0:T(8,128)S(1)} %pack.1.own_ref, f32[10,32,128]{2,1,0:T(8,128)S(1)} %collective-permute-done.2.r_ref, ...), custom_call_target="tpu_custom_call" | custom-call | tf_op jit(solution)/shard_map/krylov/pallas_call | solution.py:301
  38.7 31.8 %all_to_all.5 = f32[64,1,128]{2,1,0:T(1,128)S(1)} all-to-all(f32[64,1,128]{2,1,0:T(1,128)S(1)} %get-tuple-element.7), channel_id=1, replica_groups=mesh['groups'=4,'gx'=64] {'gx'}, dimensions={0} | all-to-all | bytes 65536 | tf_op jit(solution)/shard_map/all_to_all | solution.py:313
  70.5 1.1 %finish.1 = (f32[32,3,128]{2,1,0:T(4,128)}, f32[32,3,128]{2,1,0:T(4,128)}) custom-call(f32[15,32,128]{2,1,0:T(8,128)S(1)} %get-tuple-element.6.basis_ref, f32[8,8,128]{2,1,0:T(8,128)S(1)} %bitcast.18), custom_call_target="tpu_custom_call" | custom-call | tf_op jit(solution)/shard_map/finish/pallas_call | solution.py:315
Async XLA Ops:
  0.6 0.7 %copy-start.3 = (f32[4096]{0:T(1024)S(1)}, f32[4096]{0:T(1024)}, u32[]{:S(2)}) copy-start(f32[4096]{0:T(1024)} %param.5) | copy-start | bytes 49156
  1.3 0.9 %copy-start = (s32[6,4096]{1,0:T(8,128)S(1)}, s32[6,4096]{1,0:T(8,128)}, u32[]{:S(2)}) copy-start(s32[6,4096]{1,0:T(8,128)} %param.6) | copy-start | bytes 294916
  2.3 0.8 %copy-start.1 = (f32[3,4096]{1,0:T(4,128)S(1)}, f32[3,4096]{1,0:T(4,128)}, u32[]{:S(2)}) copy-start(f32[3,4096]{1,0:T(4,128)} %param.4) | copy-start | bytes 147460
  3.1 0.8 %copy-start.2 = (f32[3,4096]{1,0:T(4,128)S(1)}, f32[3,4096]{1,0:T(4,128)}, u32[]{:S(2)}) copy-start(f32[3,4096]{1,0:T(4,128)} %param.7) | copy-start | bytes 147460
  4.1 26.6 %collective-permute-start.3 = (f32[10,32,128]{2,1,0:T(8,128)S(1)}, f32[10,32,128]{2,1,0:T(8,128)S(1)}, u32[]{:S(2)}, u32[]{:S(2)}) collective-permute-start(f32[10,32,128]{2,1,0:T(8,128)S(1)} %pack.1.own_ref), channel_id=1, source_target_pairs={{0,62},{1,63},{2,0},{3,1},{4,2},{5,3},{6,4},{7,5},{8,6},{9,7},{10,... | collective-permute-start | bytes 491528 | tf_op jit(solution)/shard_map/ppermute | solution.py:296
  27.8 5.0 %collective-permute-start.2 = (f32[10,32,128]{2,1,0:T(8,128)S(1)}, f32[10,32,128]{2,1,0:T(8,128)S(1)}, u32[]{:S(2)}, u32[]{:S(2)}) collective-permute-start(f32[10,32,128]{2,1,0:T(8,128)S(1)} %pack.1.own_ref), channel_id=1, source_target_pairs={{0,63},{1,0},{2,1},{3,2},{4,3},{5,4},{6,5},{7,6},{8,7},{9,8},{10,9... | collective-permute-start | bytes 491528 | tf_op jit(solution)/shard_map/ppermute | solution.py:296
  28.6 4.3 %collective-permute-start.1 = (f32[10,32,128]{2,1,0:T(8,128)S(1)}, f32[10,32,128]{2,1,0:T(8,128)S(1)}, u32[]{:S(2)}, u32[]{:S(2)}) collective-permute-start(f32[10,32,128]{2,1,0:T(8,128)S(1)} %pack.1.own_ref), channel_id=1, source_target_pairs={{0,1},{1,2},{2,3},{3,4},{4,5},{5,6},{6,7},{7,8},{8,9},{9,10},{10,1... | collective-permute-start | bytes 491528 | tf_op jit(solution)/shard_map/ppermute | solution.py:296
  29.5 8.0 %collective-permute-start = (f32[10,32,128]{2,1,0:T(8,128)S(1)}, f32[10,32,128]{2,1,0:T(8,128)S(1)}, u32[]{:S(2)}, u32[]{:S(2)}) collective-permute-start(f32[10,32,128]{2,1,0:T(8,128)S(1)} %pack.1.own_ref), channel_id=1, source_target_pairs={{0,2},{1,3},{2,4},{3,5},{4,6},{5,7},{6,8},{7,9},{8,10},{9,11},{10,... | collective-permute-start | bytes 491528 | tf_op jit(solution)/shard_map/ppermute | solution.py:296

commit v2 on v1

--- a/solution.py
+++ b/solution.py
@@ -310,7 +310,10 @@
         name="krylov",
     )(far_left, left, packed, right, far_right)
 
-    everyone = lax.all_to_all(sums, "gx", split_axis=0, concat_axis=0, tiled=True)
+    order = [(i + devices // 2) % devices for i in range(devices)]
+    everyone = lax.all_to_all(
+        sums, "gx", split_axis=0, concat_axis=0, tiled=True, axis_index_groups=[order]
+    )
 
     sol, res = pl.pallas_call(
         finish_kernel,

time: 72 us -> 66.1 us (0.918)
  blocking collectives: 31.8 us -> 25.9 us
    all_to_all x1, blocking collectives: 31.8 us -> 25.9 us  [on_device(): lax.all_to_all(sums, 'gx', split_axis=0, concat_axis=0, tiled=True, axis_...]
where the time goes in v2:
time: 66.1 us; the launch traced here: 65.8 us
  blocking collectives  25.9 us (39%)
  starting transfers between devices  25.4 us (38%)
  waiting for transfers between devices  7.95 us (12%)
  local copies, waits for them, and re-layouts  3.29 us (5%)
  Pallas kernels  2.51 us (4%)
    all_to_all x1, blocking collectives, on_device(): lax.all_to_all(sums, 'gx', split_axis=0, concat_axis=0, tiled=True, axis_...  25.9 us
    ppermute x4, starting transfers between devices, moved(): return lax.ppermute(array, 'gx', pairs)  25.4 us
    ppermute x4, waiting for transfers between devices, moved(): return lax.ppermute(array, 'gx', pairs)  7.95 us
    unnamed x8, local copies, waits for them, and re-layouts  3.29 us
  transfers between devices with their start and end apart: 4, of which 4 were waited for; matrix products, arithmetic and copies ran while one was open for 0% of the time, Pallas kernels for 0%

profile of v2, /device:TPU:37, one launch (start us, length us, event | category | flops | bytes accessed | tf_op | source)
XLA Modules:
  0.0 65.8 jit_solution(17271385698885425713)
XLA Ops:
  0.6 0.0 copy-start.3
  0.6 0.7 %copy-done.3 = f32[4096]{0:T(1024)S(1)} copy-done((f32[4096]{0:T(1024)S(1)}, f32[4096]{0:T(1024)}, u32[]{:S(2)}) %copy-start.3) | copy-done | bytes 16408
  1.3 0.0 copy-start
  1.4 0.9 %copy-done = s32[6,4096]{1,0:T(8,128)S(1)} copy-done((s32[6,4096]{1,0:T(8,128)S(1)}, s32[6,4096]{1,0:T(8,128)}, u32[]{:S(2)}) %copy-start) | copy-done | bytes 98328
  2.3 0.0 copy-start.1
  2.3 0.8 %copy-done.1 = f32[3,4096]{1,0:T(4,128)S(1)} copy-done((f32[3,4096]{1,0:T(4,128)S(1)}, f32[3,4096]{1,0:T(4,128)}, u32[]{:S(2)}) %copy-start.1) | copy-done | bytes 49176
  3.1 0.0 copy-start.2
  3.1 0.8 %copy-done.2 = f32[3,4096]{1,0:T(4,128)S(1)} copy-done((f32[3,4096]{1,0:T(4,128)S(1)}, f32[3,4096]{1,0:T(4,128)}, u32[]{:S(2)}) %copy-start.2) | copy-done | bytes 49176
  3.9 0.1 pack.1.own_ref
  4.1 23.7 %collective-permute-start.3 = (f32[10,32,128]{2,1,0:T(8,128)S(1)}, f32[10,32,128]{2,1,0:T(8,128)S(1)}, u32[]{:S(2)}, u32[]{:S(2)}) collective-permute-start(f32[10,32,128]{2,1,0:T(8,128)S(1)} %pack.1.own_ref), channel_id=1, source_target_pairs={{0,62},{1,63},{2,0},{3,1},{4,2},{5,3},{6,4},{7,5},{8,6},{9,7},{10,... | collective-permute-start | bytes 491528 | tf_op jit(solution)/shard_map/ppermute | solution.py:296
  27.8 0.9 %collective-permute-start.2 = (f32[10,32,128]{2,1,0:T(8,128)S(1)}, f32[10,32,128]{2,1,0:T(8,128)S(1)}, u32[]{:S(2)}, u32[]{:S(2)}) collective-permute-start(f32[10,32,128]{2,1,0:T(8,128)S(1)} %pack.1.own_ref), channel_id=1, source_target_pairs={{0,63},{1,0},{2,1},{3,2},{4,3},{5,4},{6,5},{7,6},{8,7},{9,8},{10,9... | collective-permute-start | bytes 491528 | tf_op jit(solution)/shard_map/ppermute | solution.py:296
  28.6 0.9 %collective-permute-start.1 = (f32[10,32,128]{2,1,0:T(8,128)S(1)}, f32[10,32,128]{2,1,0:T(8,128)S(1)}, u32[]{:S(2)}, u32[]{:S(2)}) collective-permute-start(f32[10,32,128]{2,1,0:T(8,128)S(1)} %pack.1.own_ref), channel_id=1, source_target_pairs={{0,1},{1,2},{2,3},{3,4},{4,5},{5,6},{6,7},{7,8},{8,9},{9,10},{10,1... | collective-permute-start | bytes 491528 | tf_op jit(solution)/shard_map/ppermute | solution.py:296
  29.5 0.0 collective-permute-start
  29.5 1.2 %collective-permute-done.3.rr_ref = f32[10,32,128]{2,1,0:T(8,128)S(1)} collective-permute-done((f32[10,32,128]{2,1,0:T(8,128)S(1)}, f32[10,32,128]{2,1,0:T(8,128)S(1)}, u32[]{:S(2)}, u32[]{:S(2)}) %collective-permute-start.3) | collective-permute-done | bytes 163872 | tf_op jit(solution)/shard_map/ppermute | solution.py:296
  30.7 2.1 %collective-permute-done.2.r_ref = f32[10,32,128]{2,1,0:T(8,128)S(1)} collective-permute-done((f32[10,32,128]{2,1,0:T(8,128)S(1)}, f32[10,32,128]{2,1,0:T(8,128)S(1)}, u32[]{:S(2)}, u32[]{:S(2)}) %collective-permute-start.2) | collective-permute-done | bytes 163872 | tf_op jit(solution)/shard_map/ppermute | solution.py:296
  32.8 0.1 collective-permute-done.1.l_ref
  32.9 4.5 %collective-permute-done.ll_ref = f32[10,32,128]{2,1,0:T(8,128)S(1)} collective-permute-done((f32[10,32,128]{2,1,0:T(8,128)S(1)}, f32[10,32,128]{2,1,0:T(8,128)S(1)}, u32[]{:S(2)}, u32[]{:S(2)}) %collective-permute-start) | collective-permute-done | bytes 163872 | tf_op jit(solution)/shard_map/ppermute | solution.py:296
  37.5 1.2 %krylov.1 = (f32[15,32,128]{2,1,0:T(8,128)S(1)}, f32[64,1,128]{2,1,0:T(1,128)S(1)}) custom-call(f32[10,32,128]{2,1,0:T(8,128)S(1)} %collective-permute-done.ll_ref, f32[10,32,128]{2,1,0:T(8,128)S(1)} %collective-permute-done.1.l_ref, f32[10,32,128]{2,1,0:T(8,128)S(1)} %pack.1.own_ref, f32[10,32,128]{2,1,0:T(8,128)S(1)} %collective-permute-done.2.r_ref, ...), custom_call_target="tpu_custom_call" | custom-call | tf_op jit(solution)/shard_map/krylov/pallas_call | solution.py:301
  38.7 25.9 %all_to_all.5 = f32[64,1,128]{2,1,0:T(1,128)S(1)} all-to-all(f32[64,1,128]{2,1,0:T(1,128)S(1)} %get-tuple-element.7), channel_id=1, replica_groups={{32,33,34,35,36,37,38,39,40,41,42,43,44,45,46,47,48,49,50,51,52,53,54,5..., dimensions={0} | all-to-all | bytes 65536 | tf_op jit(solution)/shard_map/all_to_all | solution.py:314
  64.6 1.1 %finish.1 = (f32[32,3,128]{2,1,0:T(4,128)}, f32[32,3,128]{2,1,0:T(4,128)}) custom-call(f32[15,32,128]{2,1,0:T(8,128)S(1)} %get-tuple-element.6.basis_ref, f32[8,8,128]{2,1,0:T(8,128)S(1)} %bitcast.18), custom_call_target="tpu_custom_call" | custom-call | tf_op jit(solution)/shard_map/finish/pallas_call | solution.py:318
Async XLA Ops:
  0.6 0.7 %copy-start.3 = (f32[4096]{0:T(1024)S(1)}, f32[4096]{0:T(1024)}, u32[]{:S(2)}) copy-start(f32[4096]{0:T(1024)} %param.5) | copy-start | bytes 49156
  1.3 0.9 %copy-start = (s32[6,4096]{1,0:T(8,128)S(1)}, s32[6,4096]{1,0:T(8,128)}, u32[]{:S(2)}) copy-start(s32[6,4096]{1,0:T(8,128)} %param.6) | copy-start | bytes 294916
  2.3 0.8 %copy-start.1 = (f32[3,4096]{1,0:T(4,128)S(1)}, f32[3,4096]{1,0:T(4,128)}, u32[]{:S(2)}) copy-start(f32[3,4096]{1,0:T(4,128)} %param.4) | copy-start | bytes 147460
  3.1 0.8 %copy-start.2 = (f32[3,4096]{1,0:T(4,128)S(1)}, f32[3,4096]{1,0:T(4,128)}, u32[]{:S(2)}) copy-start(f32[3,4096]{1,0:T(4,128)} %param.7) | copy-start | bytes 147460
  4.1 26.6 %collective-permute-start.3 = (f32[10,32,128]{2,1,0:T(8,128)S(1)}, f32[10,32,128]{2,1,0:T(8,128)S(1)}, u32[]{:S(2)}, u32[]{:S(2)}) collective-permute-start(f32[10,32,128]{2,1,0:T(8,128)S(1)} %pack.1.own_ref), channel_id=1, source_target_pairs={{0,62},{1,63},{2,0},{3,1},{4,2},{5,3},{6,4},{7,5},{8,6},{9,7},{10,... | collective-permute-start | bytes 491528 | tf_op jit(solution)/shard_map/ppermute | solution.py:296
  27.8 5.0 %collective-permute-start.2 = (f32[10,32,128]{2,1,0:T(8,128)S(1)}, f32[10,32,128]{2,1,0:T(8,128)S(1)}, u32[]{:S(2)}, u32[]{:S(2)}) collective-permute-start(f32[10,32,128]{2,1,0:T(8,128)S(1)} %pack.1.own_ref), channel_id=1, source_target_pairs={{0,63},{1,0},{2,1},{3,2},{4,3},{5,4},{6,5},{7,6},{8,7},{9,8},{10,9... | collective-permute-start | bytes 491528 | tf_op jit(solution)/shard_map/ppermute | solution.py:296
  28.6 4.3 %collective-permute-start.1 = (f32[10,32,128]{2,1,0:T(8,128)S(1)}, f32[10,32,128]{2,1,0:T(8,128)S(1)}, u32[]{:S(2)}, u32[]{:S(2)}) collective-permute-start(f32[10,32,128]{2,1,0:T(8,128)S(1)} %pack.1.own_ref), channel_id=1, source_target_pairs={{0,1},{1,2},{2,3},{3,4},{4,5},{5,6},{6,7},{7,8},{8,9},{9,10},{10,1... | collective-permute-start | bytes 491528 | tf_op jit(solution)/shard_map/ppermute | solution.py:296
  29.5 8.0 %collective-permute-start = (f32[10,32,128]{2,1,0:T(8,128)S(1)}, f32[10,32,128]{2,1,0:T(8,128)S(1)}, u32[]{:S(2)}, u32[]{:S(2)}) collective-permute-start(f32[10,32,128]{2,1,0:T(8,128)S(1)} %pack.1.own_ref), channel_id=1, source_target_pairs={{0,2},{1,3},{2,4},{3,5},{4,6},{5,7},{6,8},{7,9},{8,10},{9,11},{10,... | collective-permute-start | bytes 491528 | tf_op jit(solution)/shard_map/ppermute | solution.py:296

commit v3 on v2

--- a/solution.py
+++ b/solution.py
@@ -26,23 +26,75 @@
     return value
 
 
-def pack_kernel(first_ref, pos_ref, rad_ref, nb_ref, rhs_ref, out_ref):
+def pack_kernel(first_ref, pos_hbm, rad_hbm, nb_hbm, rhs_hbm, out_ref, *scratch):
+    pos_ref, rad_ref, nb_ref, rhs_ref, sems = scratch
+    moves = [
+        pltpu.make_async_copy(src, dst, sems.at[k])
+        for k, (src, dst) in enumerate(
+            (
+                (nb_hbm, nb_ref),
+                (pos_hbm, pos_ref),
+                (rhs_hbm, rhs_ref),
+                (rad_hbm, rad_ref),
+            )
+        )
+    ]
+    for move in moves:
+        move.start()
     rows = rad_ref.shape[0]
     shape = (rows, LZ)
     ids = first_ref[0] + (
         lax.broadcasted_iota(jnp.int32, shape, 0) * LZ
         + lax.broadcasted_iota(jnp.int32, shape, 1)
     )
-    for c in range(3):
-        out_ref[c] = pos_ref[:, c, :]
-        out_ref[7 + c] = rhs_ref[:, c, :]
-    out_ref[3] = rad_ref[...]
+    for move in moves:
+        move.wait()
     slots = [nb_ref[:, s, :] - ids for s in range(nb_ref.shape[1])]
     for b, shift in enumerate((LY * LZ, LZ, 1)):
         hit = slots[0] == shift
         for other in slots[1:]:
             hit = hit | (other == shift)
         out_ref[4 + b] = jnp.where(hit, f32(1.0), f32(0.0))
+    for c in range(3):
+        out_ref[c] = pos_ref[:, c, :]
+        out_ref[7 + c] = rhs_ref[:, c, :]
+    out_ref[3] = rad_ref[...]
+
+
+def edge_kernel(own_ref, low_ref, high_ref):
+    rows = own_ref.shape[1]
+    row, lane = coordinates(rows)
+    geom = [own_ref[c] for c in range(4)]
+    inside = row < rows - 1
+    last = (row == rows - 1) & (lane == LZ - 1)
+    vector = [own_ref[7 + c] for c in range(3)]
+    bonds = all_bonds(
+        geom,
+        [own_ref[4], own_ref[5], own_ref[6]],
+        lane,
+        (None, inside, jnp.logical_not(last)),
+    )
+    push = fluxes(bonds, vector, lane, 0, rows)
+    for c in range(3):
+        low_ref[c] = geom[c][:LY]
+        high_ref[c] = geom[c][rows - LY :]
+        low_ref[4 + c] = vector[c][:LY]
+        high_ref[4 + c] = vector[c][rows - LY :]
+        low_ref[7 + c] = push[c][:LY]
+        high_ref[7 + c] = push[c][rows - LY :]
+    low_ref[3] = geom[3][:LY]
+    high_ref[3] = geom[3][rows - LY :]
+    high_ref[10] = own_ref[4, rows - LY :, :]
+    high_ref[11, : LY // 2, :] = own_ref[5, rows - LY // 2 :, :]
+    high_ref[11, LY // 2 :, :] = own_ref[6, rows - LY // 2 :, :]
+
+
+def coordinates(rows):
+    shape = (rows, LZ)
+    return (
+        lax.broadcasted_iota(jnp.int32, shape, 0),
+        lax.broadcasted_iota(jnp.int32, shape, 1),
+    )
 
 
 def up_row(x):
@@ -57,9 +109,11 @@
     return pltpu.roll(jnp.where(lane == 0, x_up, x), LZ - 1, 1)
 
 
-def bond(mask, delta, contact):
+def bond(mask, delta, contact, allowed=None):
     squared = delta[0] * delta[0] + delta[1] * delta[1] + delta[2] * delta[2]
     live = mask > 0.5
+    if allowed is not None:
+        live = live & allowed
     squared = jnp.where(live, squared, f32(1.0))
     inverse = 1.0 / (contact * jnp.sqrt(squared))
     tension = (squared * inverse - 1.0) * inverse
@@ -70,6 +124,24 @@
     return tension, [d * weight for d in delta]
 
 
+def all_bonds(geom, masks, lane, allowed=(None, None, None)):
+    total = geom[0].shape[0]
+    ahead = [g[LY:] for g in geom]
+    base = [g[: total - LY] for g in geom]
+    ups = [up_row(g) for g in geom]
+    nexts = [next_lane(g, u, lane) for g, u in zip(geom, ups)]
+
+    def build(mask, there, here, ok):
+        delta = [a - b for a, b in zip(there[:3], here[:3])]
+        return bond(mask, delta, there[3] + here[3], ok)
+
+    return (
+        build(masks[0][: total - LY], ahead, base, allowed[0]),
+        build(masks[1], ups, geom, allowed[1]),
+        build(masks[2], nexts, geom, allowed[2]),
+    )
+
+
 def flux(pair, here, there):
     tension, w = pair
     rel = [a - b for a, b in zip(here, there)]
@@ -81,81 +153,97 @@
     return [v[lo:hi] for v in values]
 
 
+def cut_pair(pair, lo, hi):
+    return pair[0][lo:hi], cut(pair[1], lo, hi)
+
+
+def side_flux(bonds, mid, up, lane, lo, hi):
+    fy = flux(cut_pair(bonds[1], lo, hi), mid, up)
+    nxt = [next_lane(x, u, lane) for x, u in zip(mid, up)]
+    fz = flux(cut_pair(bonds[2], lo, hi), mid, nxt)
+    first = lane == 0
+    result = []
+    for y, z in zip(fy, fz):
+        rolled = pltpu.roll(z, 1, 1)
+        back = down_row(y + jnp.where(first, rolled, f32(0.0)))
+        result.append(y + z - back - jnp.where(first, f32(0.0), rolled))
+    return result
+
+
+def fluxes(bonds, v, lane, lo, hi):
+    n = hi - lo
+    fx = flux(cut_pair(bonds[0], lo, hi - LY), cut(v, 0, n - LY), cut(v, LY, n))
+    side = side_flux(bonds, v, [up_row(x) for x in v], lane[:n], lo, hi)
+    result = []
+    for s, x in zip(side, fx):
+        parts = [x[:LY], -x[n - 2 * LY :]]
+        if n > 2 * LY:
+            parts.insert(1, x[LY:] - x[: n - 2 * LY])
+        result.append(s + jnp.concatenate(parts, axis=0))
+    return result
+
+
 def krylov_kernel(ll_ref, l_ref, own_ref, r_ref, rr_ref, basis_ref, sums_ref):
     rows = own_ref.shape[1]
-    depth = 2 * rows
+    depth = rows + LY
     total = rows + 2 * depth
-
-    def ext(c):
+    row, lane = coordinates(total)
+    half = LY // 2
+
+    def ext(c, low, high):
         return jnp.concatenate(
-            [ref[c] for ref in (ll_ref, l_ref, own_ref, r_ref, rr_ref)], axis=0
+            [low] + [ref[c] for ref in (l_ref, own_ref, r_ref)] + [high], axis=0
         )
 
-    lane = lax.broadcasted_iota(jnp.int32, (total, LZ), 1)
-    geom = [ext(c) for c in range(4)]
-    masks = [ext(4 + c) for c in range(3)]
-    vector = [ext(7 + c) for c in range(3)]
-
-    ahead = [g[LY:] for g in geom]
-    base = [g[: total - LY] for g in geom]
-    bond_x = bond(
-        masks[0][: total - LY],
-        [a - b for a, b in zip(ahead[:3], base[:3])],
-        ahead[3] + base[3],
-    )
-    ups = [up_row(g) for g in geom]
-    bond_y = bond(masks[1], [a - b for a, b in zip(ups[:3], geom[:3])], ups[3] + geom[3])
-    nexts = [next_lane(g, u, lane) for g, u in zip(geom, ups)]
-    bond_z = bond(
-        masks[2], [a - b for a, b in zip(nexts[:3], geom[:3])], nexts[3] + geom[3]
-    )
-
-    def pair_at(pair, lo, hi):
-        return pair[0][lo:hi], cut(pair[1], lo, hi)
+    none = jnp.zeros((LY, LZ), f32)
+    pad = jnp.zeros((LY - half, LZ), f32)
+    rim = row == LY - 1
+    past = row >= LY
+    geom = [ext(c, ll_ref[c], rr_ref[c]) for c in range(4)]
+    vector = [ext(7 + c, ll_ref[4 + c], rr_ref[4 + c]) for c in range(3)]
+    masks = [
+        ext(4, ll_ref[10], none),
+        ext(5, jnp.concatenate([pad, ll_ref[11, :half, :]], axis=0), none),
+        ext(6, jnp.concatenate([pad, ll_ref[11, half:, :]], axis=0), none),
+    ]
+    bonds = all_bonds(
+        geom, masks, lane, (None, past | rim, past | (rim & (lane == LZ - 1)))
+    )
 
     def operate(v, lo, hi):
         n = hi - lo
-        here = cut(v, 0, n - LY)
-        fx = flux(pair_at(bond_x, lo, hi - LY), here, cut(v, LY, n))
-        a, b = lo + 8, hi - 8
-        mid = cut(v, 8, n - 8)
-        up = [x[8 : n - 8] for x in (up_row(x) for x in v)]
-        ln = lane[: b - a]
-        fy = flux(pair_at(bond_y, a, b), mid, up)
-        nxt = [next_lane(x, u, ln) for x, u in zip(mid, up)]
-        fz = flux(pair_at(bond_z, a, b), mid, nxt)
-        result = []
         m = n - 2 * LY
-        for c in range(3):
-            rolled = pltpu.roll(fz[c], 1, 1)
-            first = ln == 0
-            back = down_row(fy[c] + jnp.where(first, rolled, f32(0.0)))
-            side = fy[c] + fz[c] - back - jnp.where(first, f32(0.0), rolled)
-            straight = fx[c][LY : LY + m] - fx[c][:m]
-            result.append(
-                f32(DIAGONAL_SHIFT - CENTER) * v[c][LY : LY + m]
-                + straight
-                + side[8 : 8 + m]
-            )
-        return result
-
-    own = slice(depth, depth + rows)
-    kept = [[x[own] for x in vector]]
+        fx = flux(cut_pair(bonds[0], lo, hi - LY), cut(v, 0, n - LY), cut(v, LY, n))
+        up = [up_row(x)[8 : n - 8] for x in v]
+        side = side_flux(bonds, cut(v, 8, n - 8), up, lane[: n - 16], lo + 8, hi - 8)
+        return [
+            f32(DIAGONAL_SHIFT) * v[c][LY : LY + m]
+            + (fx[c][LY : LY + m] - fx[c][:m])
+            + side[c][8 : 8 + m]
+            for c in range(3)
+        ]
+
+    kept = [cut(vector, depth, depth + rows)]
+    push = fluxes(bonds, vector, lane, 0, total)
     lo, hi = 0, total
-    before, now = None, vector
-    for k in range(ITERS):
+    before, now = vector, []
+    for c in range(3):
+        given = jnp.concatenate(
+            [ll_ref[7 + c], jnp.zeros((total - 2 * LY, LZ), f32), rr_ref[7 + c]], axis=0
+        )
+        image = f32(DIAGONAL_SHIFT - CENTER) * vector[c] + push[c] + given
+        now.append(image * f32(1.0 / RADIUS))
+    kept.append(cut(now, depth, depth + rows))
+    for k in range(1, ITERS):
         image = operate(now, lo, hi)
         m = hi - lo - 2 * LY
-        if k == 0:
-            after = [x * f32(1.0 / RADIUS) for x in image]
-        else:
-            after = [
-                x * f32(2.0 / RADIUS) - p[2 * LY : 2 * LY + m]
-                for x, p in zip(image, before)
-            ]
-        before, now = now, after
+        after = [
+            (x - f32(CENTER) * y[LY : LY + m]) * f32(2.0 / RADIUS) - p
+            for x, y, p in zip(image, now, cut(before, LY, LY + m))
+        ]
+        before, now = cut(now, LY, LY + m), after
         lo, hi = lo + LY, hi - LY
-        kept.append([x[depth - lo : depth - lo + rows] for x in now])
+        kept.append(cut(now, depth - lo, depth - lo + rows))
     for k in range(ITERS + 1):
         for c in range(3):
             basis_ref[3 * k + c] = kept[k][c]
@@ -268,6 +356,10 @@
     return array.reshape(array.shape[0], -1, LZ).transpose(1, 0, 2)
 
 
+def stay(array):
+    return pltpu.with_memory_space_constraint(array, pltpu.HBM)
+
+
 def on_device(positions, radii, neighbours, right_side):
     owned = positions.shape[1]
     rows = owned // LZ
@@ -275,20 +367,28 @@
     first = (lax.axis_index("gx") * owned).astype(jnp.int32).reshape(1)
     vmem = pl.BlockSpec(memory_space=pltpu.VMEM)
     smem = pl.BlockSpec(memory_space=pltpu.SMEM)
+    hbm = pl.BlockSpec(memory_space=pltpu.HBM)
 
     packed = pl.pallas_call(
         pack_kernel,
         out_shape=jax.ShapeDtypeStruct((10, rows, LZ), f32),
-        in_specs=[smem, vmem, vmem, vmem, vmem],
+        in_specs=[smem, hbm, hbm, hbm, hbm],
         out_specs=vmem,
+        scratch_shapes=[
+            pltpu.VMEM((rows, 3, LZ), f32),
+            pltpu.VMEM((rows, LZ), f32),
+            pltpu.VMEM((rows, neighbours.shape[0], LZ), jnp.int32),
+            pltpu.VMEM((rows, 3, LZ), f32),
+            pltpu.SemaphoreType.DMA((4,)),
+        ],
         compiler_params=pltpu.CompilerParams(vmem_limit_bytes=4 << 20),
         name="pack",
     )(
         first,
-        by_rows(positions),
-        radii.reshape(rows, LZ),
-        by_rows(neighbours),
-        by_rows(right_side),
+        stay(by_rows(positions)),
+        stay(radii.reshape(rows, LZ)),
+        stay(by_rows(neighbours)),
+        stay(by_rows(right_side)),
     )
 
     def moved(array, by):
@@ -296,7 +396,18 @@
         return lax.ppermute(array, "gx", pairs)
 
     left, right = moved(packed, 1), moved(packed, -1)
-    far_left, far_right = moved(packed, 2), moved(packed, -2)
+    low, high = pl.pallas_call(
+        edge_kernel,
+        out_shape=(
+            jax.ShapeDtypeStruct((10, LY, LZ), f32),
+            jax.ShapeDtypeStruct((12, LY, LZ), f32),
+        ),
+        in_specs=[vmem],
+        out_specs=(vmem, vmem),
+        compiler_params=pltpu.CompilerParams(vmem_limit_bytes=4 << 20),
+        name="edge",
+    )(packed)
+    far_left, far_right = moved(high, 2), moved(low, -2)
 
     basis, sums = pl.pallas_call(
         krylov_kernel,

time: 66.1 us -> 61.6 us (0.932)
  waiting for transfers between devices: 7.95 us -> 4.36 us
  local copies, waits for them, and re-layouts: 3.29 us -> 0 us
  starting transfers between devices: 25.4 us -> 26.8 us
  Pallas kernels: 2.51 us -> 3.65 us
    ppermute x4, waiting for transfers between devices: 7.95 us -> 4.36 us  [moved(): return lax.ppermute(array, 'gx', pairs)]
    unnamed x8 -> x0, local copies, waits for them, and re-layouts: 3.29 us -> none
    ppermute x4, starting transfers between devices: 25.4 us -> 26.8 us  [moved(): return lax.ppermute(array, 'gx', pairs)]
    pallas_call x1, Pallas kernels: 0.13 us -> 1.08 us  [on_device(): pl.pallas_call(pack_kernel, out_shape=jax.ShapeDtypeStruct((10, rows, LZ)...]
  transfers between devices with their start and end apart: 4 -> 4, of which waited for: 4 -> 2; matrix products, arithmetic and copies ran while one was open for 0% -> 0% of each run, Pallas kernels for 0% -> 0%
where the time goes in v3:
time: 61.6 us; the launch traced here: 61.4 us
  starting transfers between devices  26.8 us (44%)
  blocking collectives  25.9 us (42%)
  waiting for transfers between devices  4.36 us (7%)
  Pallas kernels  3.65 us (6%)
  between operations  0.67 us (1%)
    ppermute x4, starting transfers between devices, moved(): return lax.ppermute(array, 'gx', pairs)  26.8 us
    all_to_all x1, blocking collectives, on_device(): lax.all_to_all(sums, 'gx', split_axis=0, concat_axis=0, tiled=True, axis_...  25.9 us
    ppermute x4, waiting for transfers between devices, moved(): return lax.ppermute(array, 'gx', pairs)  4.36 us
  transfers between devices with their start and end apart: 4, of which 2 were waited for; matrix products, arithmetic and copies ran while one was open for 0% of the time, Pallas kernels for 0%

profile of v3, /device:TPU:37, one launch (start us, length us, event | category | flops | bytes accessed | tf_op | source)
XLA Modules:
  0.0 61.4 jit_solution(15907332391360287834)
XLA Ops:
  0.6 1.1 %pack.1.own_ref = f32[10,32,128]{2,1,0:T(8,128)S(1)} custom-call(s32[1]{0:T(128)} %bitcast.first_ref, f32[32,3,128]{2,1,0:T(4,128)} %bitcast.20, f32[32,128]{1,0:T(8,128)} %bitcast.22, s32[32,6,128]{2,1,0:T(8,128)} %bitcast.19, f32[32,3,128]{2,1,0:T(4,128)} %bitcast.21), custom_call_target="tpu_custom_call" | custom-call | tf_op jit(solution)/shard_map/pack/pallas_call | solution.py:372
  1.7 20.5 %collective-permute-start.2 = (f32[10,32,128]{2,1,0:T(8,128)S(1)}, f32[10,32,128]{2,1,0:T(8,128)S(1)}, u32[]{:S(2)}, u32[]{:S(2)}) collective-permute-start(f32[10,32,128]{2,1,0:T(8,128)S(1)} %pack.1.own_ref), channel_id=1, source_target_pairs={{0,63},{1,0},{2,1},{3,2},{4,3},{5,4},{6,5},{7,6},{8,7},{9,8},{10,9... | collective-permute-start | bytes 491528 | tf_op jit(solution)/shard_map/ppermute | solution.py:396
  22.2 0.0 collective-permute-start.1
  22.2 0.2 edge.1
  22.4 0.1 collective-permute-start
  22.5 6.2 %collective-permute-start.3 = (f32[10,16,128]{2,1,0:T(8,128)S(1)}, f32[10,16,128]{2,1,0:T(8,128)S(1)}, u32[]{:S(2)}, u32[]{:S(2)}) collective-permute-start(f32[10,16,128]{2,1,0:T(8,128)S(1)} %get-tuple-element.9), channel_id=1, source_target_pairs={{0,62},{1,63},{2,0},{3,1},{4,2},{5,3},{6,4},{7,5},{8,6},{9,7},{10,... | collective-permute-start | bytes 245768 | tf_op jit(solution)/shard_map/ppermute | solution.py:396
  28.8 1.5 %collective-permute-done.3.rr_ref = f32[10,16,128]{2,1,0:T(8,128)S(1)} collective-permute-done((f32[10,16,128]{2,1,0:T(8,128)S(1)}, f32[10,16,128]{2,1,0:T(8,128)S(1)}, u32[]{:S(2)}, u32[]{:S(2)}) %collective-permute-start.3) | collective-permute-done | bytes 81952 | tf_op jit(solution)/shard_map/ppermute | solution.py:396
  30.2 2.9 %collective-permute-done.ll_ref = f32[12,16,128]{2,1,0:T(8,128)S(1)} collective-permute-done((f32[12,16,128]{2,1,0:T(8,128)S(1)}, f32[12,16,128]{2,1,0:T(8,128)S(1)}, u32[]{:S(2)}, u32[]{:S(2)}) %collective-permute-start) | collective-permute-done | bytes 98336 | tf_op jit(solution)/shard_map/ppermute | solution.py:396
  33.1 0.0 collective-permute-done.2.r_ref
  33.1 0.0 collective-permute-done.1.l_ref
  33.1 1.2 %krylov.1 = (f32[15,32,128]{2,1,0:T(8,128)S(1)}, f32[64,1,128]{2,1,0:T(1,128)S(1)}) custom-call(f32[12,16,128]{2,1,0:T(8,128)S(1)} %collective-permute-done.ll_ref, f32[10,32,128]{2,1,0:T(8,128)S(1)} %collective-permute-done.1.l_ref, f32[10,32,128]{2,1,0:T(8,128)S(1)} %pack.1.own_ref, f32[10,32,128]{2,1,0:T(8,128)S(1)} %collective-permute-done.2.r_ref, ...), custom_call_target="tpu_custom_call" | custom-call | tf_op jit(solution)/shard_map/krylov/pallas_call | solution.py:412
  34.3 25.9 %all_to_all.5 = f32[64,1,128]{2,1,0:T(1,128)S(1)} all-to-all(f32[64,1,128]{2,1,0:T(1,128)S(1)} %get-tuple-element.11), channel_id=1, replica_groups={{32,33,34,35,36,37,38,39,40,41,42,43,44,45,46,47,48,49,50,51,52,53,54,5..., dimensions={0} | all-to-all | bytes 65536 | tf_op jit(solution)/shard_map/all_to_all | solution.py:425
  60.3 1.1 %finish.1 = (f32[32,3,128]{2,1,0:T(4,128)}, f32[32,3,128]{2,1,0:T(4,128)}) custom-call(f32[15,32,128]{2,1,0:T(8,128)S(1)} %get-tuple-element.10.basis_ref, f32[8,8,128]{2,1,0:T(8,128)S(1)} %bitcast.18), custom_call_target="tpu_custom_call" | custom-call | tf_op jit(solution)/shard_map/finish/pallas_call | solution.py:429
Async XLA Ops:
  1.7 31.4 %collective-permute-start.2 = (f32[10,32,128]{2,1,0:T(8,128)S(1)}, f32[10,32,128]{2,1,0:T(8,128)S(1)}, u32[]{:S(2)}, u32[]{:S(2)}) collective-permute-start(f32[10,32,128]{2,1,0:T(8,128)S(1)} %pack.1.own_ref), channel_id=1, source_target_pairs={{0,63},{1,0},{2,1},{3,2},{4,3},{5,4},{6,5},{7,6},{8,7},{9,8},{10,9... | collective-permute-start | bytes 491528 | tf_op jit(solution)/shard_map/ppermute | solution.py:396
  22.2 10.9 %collective-permute-start.1 = (f32[10,32,128]{2,1,0:T(8,128)S(1)}, f32[10,32,128]{2,1,0:T(8,128)S(1)}, u32[]{:S(2)}, u32[]{:S(2)}) collective-permute-start(f32[10,32,128]{2,1,0:T(8,128)S(1)} %pack.1.own_ref), channel_id=1, source_target_pairs={{0,1},{1,2},{2,3},{3,4},{4,5},{5,6},{6,7},{7,8},{8,9},{9,10},{10,1... | collective-permute-start | bytes 491528 | tf_op jit(solution)/shard_map/ppermute | solution.py:396
  22.4 10.7 %collective-permute-start = (f32[12,16,128]{2,1,0:T(8,128)S(1)}, f32[12,16,128]{2,1,0:T(8,128)S(1)}, u32[]{:S(2)}, u32[]{:S(2)}) collective-permute-start(f32[12,16,128]{2,1,0:T(8,128)S(1)} %get-tuple-element.8), channel_id=1, source_target_pairs={{0,2},{1,3},{2,4},{3,5},{4,6},{5,7},{6,8},{7,9},{8,10},{9,11},{10,... | collective-permute-start | bytes 294920 | tf_op jit(solution)/shard_map/ppermute | solution.py:396
  22.5 7.7 %collective-permute-start.3 = (f32[10,16,128]{2,1,0:T(8,128)S(1)}, f32[10,16,128]{2,1,0:T(8,128)S(1)}, u32[]{:S(2)}, u32[]{:S(2)}) collective-permute-start(f32[10,16,128]{2,1,0:T(8,128)S(1)} %get-tuple-element.9), channel_id=1, source_target_pairs={{0,62},{1,63},{2,0},{3,1},{4,2},{5,3},{6,4},{7,5},{8,6},{9,7},{10,... | collective-permute-start | bytes 245768 | tf_op jit(solution)/shard_map/ppermute | solution.py:396

commit v4 on v3

--- a/solution.py
+++ b/solution.py
@@ -4,6 +4,7 @@
 from jax.experimental import pallas as pl
 from jax.experimental.pallas import tpu as pltpu
 from jax.sharding import PartitionSpec as P
+
 
 LY = 16
 LZ = 128
@@ -183,17 +184,21 @@
     return result
 
 
-def krylov_kernel(ll_ref, l_ref, own_ref, r_ref, rr_ref, basis_ref, sums_ref):
+def krylov_kernel(
+    odd_ref, ll_ref, far_ref, own_ref, mate_ref, rr_ref, basis_ref, sums_ref
+):
     rows = own_ref.shape[1]
+    odd = odd_ref[0] == 1
     depth = rows + LY
     total = rows + 2 * depth
     row, lane = coordinates(total)
     half = LY // 2
 
     def ext(c, low, high):
-        return jnp.concatenate(
-            [low] + [ref[c] for ref in (l_ref, own_ref, r_ref)] + [high], axis=0
-        )
+        outer, mate = far_ref[c], mate_ref[c]
+        left = jnp.where(odd, mate, outer)
+        right = jnp.where(odd, outer, mate)
+        return jnp.concatenate([low, left, own_ref[c], right, high], axis=0)
 
     none = jnp.zeros((LY, LZ), f32)
     pad = jnp.zeros((LY - half, LZ), f32)
@@ -234,7 +239,7 @@
         image = f32(DIAGONAL_SHIFT - CENTER) * vector[c] + push[c] + given
         now.append(image * f32(1.0 / RADIUS))
     kept.append(cut(now, depth, depth + rows))
-    for k in range(1, ITERS):
+    for _ in range(1, ITERS):
         image = operate(now, lo, hi)
         m = hi - lo - 2 * LY
         after = [
@@ -268,7 +273,7 @@
     line = jnp.where(col // 16 == sub, line, f32(0.0))
     for s in (4, 2, 1):
         line = line + pltpu.roll(line, s, 0)
-    sums_ref[...] = jnp.broadcast_to(line[:1][None], sums_ref.shape)
+    sums_ref[...] = line[:1]
 
 
 def coefficients(products):
@@ -364,7 +369,9 @@
     owned = positions.shape[1]
     rows = owned // LZ
     devices = lax.axis_size("gx")
-    first = (lax.axis_index("gx") * owned).astype(jnp.int32).reshape(1)
+    place = lax.axis_index("gx").astype(jnp.int32)
+    first = (place * owned).reshape(1)
+    odd = (place % 2).reshape(1)
     vmem = pl.BlockSpec(memory_space=pltpu.VMEM)
     smem = pl.BlockSpec(memory_space=pltpu.SMEM)
     hbm = pl.BlockSpec(memory_space=pltpu.HBM)
@@ -391,11 +398,9 @@
         stay(by_rows(right_side)),
     )
 
-    def moved(array, by):
-        pairs = [(i, (i + by) % devices) for i in range(devices)]
-        return lax.ppermute(array, "gx", pairs)
-
-    left, right = moved(packed, 1), moved(packed, -1)
+    def moved(array, to):
+        return lax.ppermute(array, "gx", [(i, to(i) % devices) for i in range(devices)])
+
     low, high = pl.pallas_call(
         edge_kernel,
         out_shape=(
@@ -407,23 +412,33 @@
         compiler_params=pltpu.CompilerParams(vmem_limit_bytes=4 << 20),
         name="edge",
     )(packed)
-    far_left, far_right = moved(high, 2), moved(low, -2)
+    across = moved(packed, lambda i: i + 1 if i % 2 else i - 1)
+    far_left = moved(high, lambda i: i + 2)
+    far_right = moved(low, lambda i: i - 2)
+    mate = moved(packed, lambda i: i ^ 1)
 
     basis, sums = pl.pallas_call(
         krylov_kernel,
         out_shape=(
             jax.ShapeDtypeStruct((3 * (ITERS + 1), rows, LZ), f32),
-            jax.ShapeDtypeStruct((devices, 1, LZ), f32),
+            jax.ShapeDtypeStruct((1, LZ), f32),
         ),
-        in_specs=[vmem] * 5,
+        in_specs=[smem] + [vmem] * 5,
         out_specs=(vmem, vmem),
         compiler_params=pltpu.CompilerParams(vmem_limit_bytes=12 << 20),
         name="krylov",
-    )(far_left, left, packed, right, far_right)
-
-    order = [(i + devices // 2) % devices for i in range(devices)]
+    )(odd, far_left, across, packed, mate, far_right)
+
+    chips = devices // 2
+    sums = sums + moved(sums, lambda i: i ^ 1)
+    groups = [[2 * ((z + chips // 2) % chips) + c for z in range(chips)] for c in (0, 1)]
     everyone = lax.all_to_all(
-        sums, "gx", split_axis=0, concat_axis=0, tiled=True, axis_index_groups=[order]
+        jnp.broadcast_to(sums[None], (chips, 1, LZ)),
+        "gx",
+        split_axis=0,
+        concat_axis=0,
+        tiled=True,
+        axis_index_groups=groups,
     )
 
     sol, res = pl.pallas_call(

time: 61.6 us -> 59.8 us (0.971)
  blocking collectives: 25.9 us -> 23.5 us
    all_to_all x1, blocking collectives: 25.9 us -> 23.5 us  [on_device(): lax.all_to_all(jnp.broadcast_to(sums[None], (chips, 1, LZ)), 'gx', split_...]
    ppermute x4 -> x5, starting transfers between devices: 26.8 us -> 27.3 us  [moved(): lax.ppermute(array, 'gx', [(i, to(i) % devices) for i in range(devices)])]
    ppermute x4 -> x5, waiting for transfers between devices: 4.36 us -> 4.12 us  [moved(): lax.ppermute(array, 'gx', [(i, to(i) % devices) for i in range(devices)])]
  transfers between devices with their start and end apart: 4 -> 5, of which waited for: 2 -> 3; matrix products, arithmetic and copies ran while one was open for 0% -> 0% of each run, Pallas kernels for 0% -> 0%
where the time goes in v4:
time: 59.8 us; the launch traced here: 59.3 us
  starting transfers between devices  27.3 us (46%)
  blocking collectives  23.5 us (39%)
  waiting for transfers between devices  4.12 us (7%)
  Pallas kernels  3.65 us (6%)
  between operations  0.67 us (1%)
    ppermute x5, starting transfers between devices, moved(): lax.ppermute(array, 'gx', [(i, to(i) % devices) for i in range(devices)])  27.3 us
    all_to_all x1, blocking collectives, on_device(): lax.all_to_all(jnp.broadcast_to(sums[None], (chips, 1, LZ)), 'gx', split_...  23.5 us
    ppermute x5, waiting for transfers between devices, moved(): lax.ppermute(array, 'gx', [(i, to(i) % devices) for i in range(devices)])  4.12 us
    pallas_call x1, Pallas kernels, on_device(): pl.pallas_call(krylov_kernel, out_shape=(jax.ShapeDtypeStruct((3 * (ITERS...  1.23 us
  transfers between devices with their start and end apart: 5, of which 3 were waited for; matrix products, arithmetic and copies ran while one was open for 0% of the time, Pallas kernels for 0%

profile of v4, /device:TPU:37, one launch (start us, length us, event | category | flops | bytes accessed | tf_op | source)
XLA Modules:
  0.0 59.3 jit_solution(14607975846570364377)
XLA Ops:
  0.6 1.1 %pack.1.own_ref = f32[10,32,128]{2,1,0:T(8,128)S(1)} custom-call(s32[1]{0:T(128)} %bitcast.1.first_ref, f32[32,3,128]{2,1,0:T(4,128)} %bitcast.23, f32[32,128]{1,0:T(8,128)} %bitcast.25, s32[32,6,128]{2,1,0:T(8,128)} %bitcast.22, f32[32,3,128]{2,1,0:T(4,128)} %bitcast.24), custom_call_target="tpu_custom_call" | custom-call | tf_op jit(solution)/shard_map/pack/pallas_call | solution.py:379
  1.7 20.5 %collective-permute-start.2 = (f32[10,32,128]{2,1,0:T(8,128)S(1)}, f32[10,32,128]{2,1,0:T(8,128)S(1)}, u32[]{:S(2)}, u32[]{:S(2)}) collective-permute-start(f32[10,32,128]{2,1,0:T(8,128)S(1)} %pack.1.own_ref), channel_id=1, source_target_pairs={{0,1},{1,0},{2,3},{3,2},{4,5},{5,4},{6,7},{7,6},{8,9},{9,8},{10,11... | collective-permute-start | bytes 491528 | tf_op jit(solution)/shard_map/ppermute | solution.py:402
  22.3 0.0 collective-permute-start.1
  22.3 0.2 edge.1
  22.5 0.1 collective-permute-start
  22.6 3.9 %collective-permute-start.3 = (f32[10,16,128]{2,1,0:T(8,128)S(1)}, f32[10,16,128]{2,1,0:T(8,128)S(1)}, u32[]{:S(2)}, u32[]{:S(2)}) collective-permute-start(f32[10,16,128]{2,1,0:T(8,128)S(1)} %get-tuple-element.9), channel_id=1, source_target_pairs={{0,62},{1,63},{2,0},{3,1},{4,2},{5,3},{6,4},{7,5},{8,6},{9,7},{10,... | collective-permute-start | bytes 245768 | tf_op jit(solution)/shard_map/ppermute | solution.py:402
  26.5 2.1 %collective-permute-done.3.rr_ref = f32[10,16,128]{2,1,0:T(8,128)S(1)} collective-permute-done((f32[10,16,128]{2,1,0:T(8,128)S(1)}, f32[10,16,128]{2,1,0:T(8,128)S(1)}, u32[]{:S(2)}, u32[]{:S(2)}) %collective-permute-start.3) | collective-permute-done | bytes 81952 | tf_op jit(solution)/shard_map/ppermute | solution.py:402
  28.6 1.2 %collective-permute-done.ll_ref = f32[12,16,128]{2,1,0:T(8,128)S(1)} collective-permute-done((f32[12,16,128]{2,1,0:T(8,128)S(1)}, f32[12,16,128]{2,1,0:T(8,128)S(1)}, u32[]{:S(2)}, u32[]{:S(2)}) %collective-permute-start) | collective-permute-done | bytes 98336 | tf_op jit(solution)/shard_map/ppermute | solution.py:402
  29.8 0.0 collective-permute-done.2.mate_ref
  29.8 0.0 collective-permute-done.1.far_ref
  29.8 1.2 %krylov.1 = (f32[15,32,128]{2,1,0:T(8,128)S(1)}, f32[1,128]{1,0:T(1,128)S(1)}) custom-call(s32[1]{0:T(128)} %bitcast.odd_ref, f32[12,16,128]{2,1,0:T(8,128)S(1)} %collective-permute-done.ll_ref, f32[10,32,128]{2,1,0:T(8,128)S(1)} %collective-permute-done.1.far_ref, f32[10,32,128]{2,1,0:T(8,128)S(1)} %pack.1.own_ref, ...), custom_call_target="tpu_custom_call" | custom-call | tf_op jit(solution)/shard_map/krylov/pallas_call | solution.py:420
  31.0 2.8 %collective-permute-start.4 = (f32[1,128]{1,0:T(1,128)S(1)}, f32[1,128]{1,0:T(1,128)S(1)}, u32[]{:S(2)}, u32[]{:S(2)}) collective-permute-start(f32[1,128]{1,0:T(1,128)S(1)} %get-tuple-element.11), channel_id=1, source_target_pairs={{0,1},{1,0},{2,3},{3,2},{4,5},{5,4},{6,7},{7,6},{8,9},{9,8},{10,11... | collective-permute-start | bytes 1544 | tf_op jit(solution)/shard_map/ppermute | solution.py:402
  33.8 0.8 %collective-permute-done.4 = f32[1,128]{1,0:T(1,128)S(1)} collective-permute-done((f32[1,128]{1,0:T(1,128)S(1)}, f32[1,128]{1,0:T(1,128)S(1)}, u32[]{:S(2)}, u32[]{:S(2)}) %collective-permute-start.4) | collective-permute-done | bytes 544 | tf_op jit(solution)/shard_map/ppermute | solution.py:402
  34.6 23.5 %all_to_all.5 = f32[32,1,128]{2,1,0:T(1,128)S(1)} all-to-all(f32[32,1,128]{2,1,0:T(1,128)S(1)} %broadcast_in_dim.9), channel_id=1, replica_groups={{32,34,36,38,40,42,44,46,48,50,52,54,56,58,60,62,0,2,4,6,8,10,12,14,16,..., dimensions={0} | all-to-all | bytes 32768 | tf_op jit(solution)/shard_map/all_to_all | solution.py:435
  58.2 1.1 %finish.1 = (f32[32,3,128]{2,1,0:T(4,128)}, f32[32,3,128]{2,1,0:T(4,128)}) custom-call(f32[15,32,128]{2,1,0:T(8,128)S(1)} %get-tuple-element.10.basis_ref, f32[4,8,128]{2,1,0:T(8,128)S(1)} %bitcast.21), custom_call_target="tpu_custom_call" | custom-call | tf_op jit(solution)/shard_map/finish/pallas_call | solution.py:444
  (2 shorter events, 0.0 us)
Async XLA Ops:
  1.7 28.1 %collective-permute-start.2 = (f32[10,32,128]{2,1,0:T(8,128)S(1)}, f32[10,32,128]{2,1,0:T(8,128)S(1)}, u32[]{:S(2)}, u32[]{:S(2)}) collective-permute-start(f32[10,32,128]{2,1,0:T(8,128)S(1)} %pack.1.own_ref), channel_id=1, source_target_pairs={{0,1},{1,0},{2,3},{3,2},{4,5},{5,4},{6,7},{7,6},{8,9},{9,8},{10,11... | collective-permute-start | bytes 491528 | tf_op jit(solution)/shard_map/ppermute | solution.py:402
  22.3 7.5 %collective-permute-start.1 = (f32[10,32,128]{2,1,0:T(8,128)S(1)}, f32[10,32,128]{2,1,0:T(8,128)S(1)}, u32[]{:S(2)}, u32[]{:S(2)}) collective-permute-start(f32[10,32,128]{2,1,0:T(8,128)S(1)} %pack.1.own_ref), channel_id=1, source_target_pairs={{0,63},{1,2},{2,1},{3,4},{4,3},{5,6},{6,5},{7,8},{8,7},{9,10},{10,... | collective-permute-start | bytes 491528 | tf_op jit(solution)/shard_map/ppermute | solution.py:402
  22.5 7.3 %collective-permute-start = (f32[12,16,128]{2,1,0:T(8,128)S(1)}, f32[12,16,128]{2,1,0:T(8,128)S(1)}, u32[]{:S(2)}, u32[]{:S(2)}) collective-permute-start(f32[12,16,128]{2,1,0:T(8,128)S(1)} %get-tuple-element.8), channel_id=1, source_target_pairs={{0,2},{1,3},{2,4},{3,5},{4,6},{5,7},{6,8},{7,9},{8,10},{9,11},{10,... | collective-permute-start | bytes 294920 | tf_op jit(solution)/shard_map/ppermute | solution.py:402
  22.6 6.0 %collective-permute-start.3 = (f32[10,16,128]{2,1,0:T(8,128)S(1)}, f32[10,16,128]{2,1,0:T(8,128)S(1)}, u32[]{:S(2)}, u32[]{:S(2)}) collective-permute-start(f32[10,16,128]{2,1,0:T(8,128)S(1)} %get-tuple-element.9), channel_id=1, source_target_pairs={{0,62},{1,63},{2,0},{3,1},{4,2},{5,3},{6,4},{7,5},{8,6},{9,7},{10,... | collective-permute-start | bytes 245768 | tf_op jit(solution)/shard_map/ppermute | solution.py:402
  31.0 3.6 %collective-permute-start.4 = (f32[1,128]{1,0:T(1,128)S(1)}, f32[1,128]{1,0:T(1,128)S(1)}, u32[]{:S(2)}, u32[]{:S(2)}) collective-permute-start(f32[1,128]{1,0:T(1,128)S(1)} %get-tuple-element.11), channel_id=1, source_target_pairs={{0,1},{1,0},{2,3},{3,2},{4,5},{5,4},{6,7},{7,6},{8,9},{9,8},{10,11... | collective-permute-start | bytes 1544 | tf_op jit(solution)/shard_map/ppermute | solution.py:402

commit v5 on v4

--- a/solution.py
+++ b/solution.py
@@ -116,10 +116,11 @@
     if allowed is not None:
         live = live & allowed
     squared = jnp.where(live, squared, f32(1.0))
-    inverse = 1.0 / (contact * jnp.sqrt(squared))
-    tension = (squared * inverse - 1.0) * inverse
-    over = inverse * contact
-    weight = jnp.sqrt(inverse) * over
+    shrink = lax.rsqrt(squared)
+    inverse = 1.0 / (contact * (squared * shrink))
+    scaled = inverse * f32(2.0 / RADIUS)
+    tension = (squared * inverse - 1.0) * scaled
+    weight = (scaled * lax.rsqrt(scaled)) * shrink
     tension = jnp.where(live, tension, f32(0.0))
     weight = jnp.where(live, weight, f32(0.0))
     return tension, [d * weight for d in delta]
@@ -219,10 +220,11 @@
         n = hi - lo
         m = n - 2 * LY
         fx = flux(cut_pair(bonds[0], lo, hi - LY), cut(v, 0, n - LY), cut(v, LY, n))
-        up = [up_row(x)[8 : n - 8] for x in v]
-        side = side_flux(bonds, cut(v, 8, n - 8), up, lane[: n - 16], lo + 8, hi - 8)
+        up = [up_row(x[8 : n - 8])[: n - 24] for x in v]
+        mid = cut(v, 8, n - LY)
+        side = side_flux(bonds, mid, up, lane[: n - 24], lo + 8, hi - LY)
         return [
-            f32(DIAGONAL_SHIFT) * v[c][LY : LY + m]
+            f32(2.0 * (DIAGONAL_SHIFT - CENTER) / RADIUS) * v[c][LY : LY + m]
             + (fx[c][LY : LY + m] - fx[c][:m])
             + side[c][8 : 8 + m]
             for c in range(3)
@@ -236,16 +238,13 @@
         given = jnp.concatenate(
             [ll_ref[7 + c], jnp.zeros((total - 2 * LY, LZ), f32), rr_ref[7 + c]], axis=0
         )
-        image = f32(DIAGONAL_SHIFT - CENTER) * vector[c] + push[c] + given
-        now.append(image * f32(1.0 / RADIUS))
+        image = f32(2.0 * (DIAGONAL_SHIFT - CENTER) / RADIUS) * vector[c]
+        now.append(f32(0.5) * (image + push[c] + given))
     kept.append(cut(now, depth, depth + rows))
     for _ in range(1, ITERS):
         image = operate(now, lo, hi)
         m = hi - lo - 2 * LY
-        after = [
-            (x - f32(CENTER) * y[LY : LY + m]) * f32(2.0 / RADIUS) - p
-            for x, y, p in zip(image, now, cut(before, LY, LY + m))
-        ]
+        after = [x - p for x, p in zip(image, cut(before, LY, LY + m))]
         before, now = cut(now, LY, LY + m), after
         lo, hi = lo + LY, hi - LY
         kept.append(cut(now, depth - lo, depth - lo + rows))
@@ -332,7 +331,9 @@
     return res, sol
 
 
-def finish_kernel(basis_ref, sums_ref, sol_ref, res_ref):
+def finish_kernel(
+    basis_ref, sums_ref, sol_hbm, res_hbm, sol_ref, res_ref, sems
+):
     line = jnp.sum(sums_ref[...], axis=0)
     line = jnp.sum(line, axis=0, keepdims=True)
     line = jnp.broadcast_to(line, (8, LZ))
@@ -344,17 +345,25 @@
     ]
     res, sol = coefficients(products)
     rows = basis_ref.shape[1]
-    for c in range(3):
-        for r in range(0, rows, 8):
-            t = [basis_ref[3 * k + c, r : r + 8, :] for k in range(ITERS + 1)]
-            x = sol[0] * t[0]
-            for k in range(1, ITERS):
-                x = x + sol[k] * t[k]
-            y = res[0] * t[0]
-            for k in range(1, ITERS + 1):
-                y = y + res[k] * t[k]
-            sol_ref[r : r + 8, c, :] = x
-            res_ref[r : r + 8, c, :] = y
+
+    def combine(weights, to_ref):
+        for c in range(3):
+            for r in range(0, rows, 8):
+                x = weights[0] * basis_ref[c, r : r + 8, :]
+                for k in range(1, len(weights)):
+                    x = x + weights[k] * basis_ref[3 * k + c, r : r + 8, :]
+                to_ref[r : r + 8, c, :] = x
+
+    leave = [
+        pltpu.make_async_copy(sol_ref, sol_hbm, sems.at[0]),
+        pltpu.make_async_copy(res_ref, res_hbm, sems.at[1]),
+    ]
+    combine(res, res_ref)
+    leave[1].start()
+    combine(sol, sol_ref)
+    leave[0].start()
+    leave[1].wait()
+    leave[0].wait()
 
 
 def by_rows(array):
@@ -448,7 +457,12 @@
             jax.ShapeDtypeStruct((rows, 3, LZ), f32),
         ),
         in_specs=[vmem, vmem],
-        out_specs=(vmem, vmem),
+        out_specs=(hbm, hbm),
+        scratch_shapes=[
+            pltpu.VMEM((rows, 3, LZ), f32),
+            pltpu.VMEM((rows, 3, LZ), f32),
+            pltpu.SemaphoreType.DMA((2,)),
+        ],
         compiler_params=pltpu.CompilerParams(vmem_limit_bytes=4 << 20),
         name="finish",
     )(basis, everyone.reshape(-1, 8, LZ))

time: 59.8 us -> 59.7 us (level)
  no operation moved by 1% of the time
where the time goes in v5:
time: 59.7 us; the launch traced here: 59.2 us
  starting transfers between devices  27.3 us (46%)
  blocking collectives  23.5 us (39%)
  waiting for transfers between devices  4.12 us (7%)
  Pallas kernels  3.58 us (6%)
  between operations  0.67 us (1%)
    ppermute x5, starting transfers between devices, moved(): lax.ppermute(array, 'gx', [(i, to(i) % devices) for i in range(devices)])  27.3 us
    all_to_all x1, blocking collectives, on_device(): lax.all_to_all(jnp.broadcast_to(sums[None], (chips, 1, LZ)), 'gx', split_...  23.5 us
    ppermute x5, waiting for transfers between devices, moved(): lax.ppermute(array, 'gx', [(i, to(i) % devices) for i in range(devices)])  4.12 us
  transfers between devices with their start and end apart: 5, of which 3 were waited for; matrix products, arithmetic and copies ran while one was open for 0% of the time, Pallas kernels for 0%

profile of v5, /device:TPU:37, one launch (start us, length us, event | category | flops | bytes accessed | tf_op | source)
XLA Modules:
  0.0 59.2 jit_solution(15444894715378288507)
XLA Ops:
  0.6 1.1 %pack.1.own_ref = f32[10,32,128]{2,1,0:T(8,128)S(1)} custom-call(s32[1]{0:T(128)} %bitcast.1.first_ref, f32[32,3,128]{2,1,0:T(4,128)} %bitcast.23, f32[32,128]{1,0:T(8,128)} %bitcast.25, s32[32,6,128]{2,1,0:T(8,128)} %bitcast.22, f32[32,3,128]{2,1,0:T(4,128)} %bitcast.24), custom_call_target="tpu_custom_call" | custom-call | tf_op jit(solution)/shard_map/pack/pallas_call | solution.py:388
  1.7 20.5 %collective-permute-start.2 = (f32[10,32,128]{2,1,0:T(8,128)S(1)}, f32[10,32,128]{2,1,0:T(8,128)S(1)}, u32[]{:S(2)}, u32[]{:S(2)}) collective-permute-start(f32[10,32,128]{2,1,0:T(8,128)S(1)} %pack.1.own_ref), channel_id=1, source_target_pairs={{0,1},{1,0},{2,3},{3,2},{4,5},{5,4},{6,7},{7,6},{8,9},{9,8},{10,11... | collective-permute-start | bytes 491528 | tf_op jit(solution)/shard_map/ppermute | solution.py:411
  22.3 0.0 collective-permute-start.1
  22.3 0.2 edge.1
  22.5 0.1 collective-permute-start
  22.6 3.9 %collective-permute-start.3 = (f32[10,16,128]{2,1,0:T(8,128)S(1)}, f32[10,16,128]{2,1,0:T(8,128)S(1)}, u32[]{:S(2)}, u32[]{:S(2)}) collective-permute-start(f32[10,16,128]{2,1,0:T(8,128)S(1)} %get-tuple-element.9), channel_id=1, source_target_pairs={{0,62},{1,63},{2,0},{3,1},{4,2},{5,3},{6,4},{7,5},{8,6},{9,7},{10,... | collective-permute-start | bytes 245768 | tf_op jit(solution)/shard_map/ppermute | solution.py:411
  26.5 2.1 %collective-permute-done.3.rr_ref = f32[10,16,128]{2,1,0:T(8,128)S(1)} collective-permute-done((f32[10,16,128]{2,1,0:T(8,128)S(1)}, f32[10,16,128]{2,1,0:T(8,128)S(1)}, u32[]{:S(2)}, u32[]{:S(2)}) %collective-permute-start.3) | collective-permute-done | bytes 81952 | tf_op jit(solution)/shard_map/ppermute | solution.py:411
  28.6 1.2 %collective-permute-done.ll_ref = f32[12,16,128]{2,1,0:T(8,128)S(1)} collective-permute-done((f32[12,16,128]{2,1,0:T(8,128)S(1)}, f32[12,16,128]{2,1,0:T(8,128)S(1)}, u32[]{:S(2)}, u32[]{:S(2)}) %collective-permute-start) | collective-permute-done | bytes 98336 | tf_op jit(solution)/shard_map/ppermute | solution.py:411
  29.8 0.0 collective-permute-done.2.mate_ref
  29.8 0.0 collective-permute-done.1.far_ref
  29.8 1.2 %krylov.1 = (f32[15,32,128]{2,1,0:T(8,128)S(1)}, f32[1,128]{1,0:T(1,128)S(1)}) custom-call(s32[1]{0:T(128)} %bitcast.odd_ref, f32[12,16,128]{2,1,0:T(8,128)S(1)} %collective-permute-done.ll_ref, f32[10,32,128]{2,1,0:T(8,128)S(1)} %collective-permute-done.1.far_ref, f32[10,32,128]{2,1,0:T(8,128)S(1)} %pack.1.own_ref, ...), custom_call_target="tpu_custom_call" | custom-call | tf_op jit(solution)/shard_map/krylov/pallas_call | solution.py:429
  31.0 2.8 %collective-permute-start.4 = (f32[1,128]{1,0:T(1,128)S(1)}, f32[1,128]{1,0:T(1,128)S(1)}, u32[]{:S(2)}, u32[]{:S(2)}) collective-permute-start(f32[1,128]{1,0:T(1,128)S(1)} %get-tuple-element.11), channel_id=1, source_target_pairs={{0,1},{1,0},{2,3},{3,2},{4,5},{5,4},{6,7},{7,6},{8,9},{9,8},{10,11... | collective-permute-start | bytes 1544 | tf_op jit(solution)/shard_map/ppermute | solution.py:411
  33.7 0.8 %collective-permute-done.4 = f32[1,128]{1,0:T(1,128)S(1)} collective-permute-done((f32[1,128]{1,0:T(1,128)S(1)}, f32[1,128]{1,0:T(1,128)S(1)}, u32[]{:S(2)}, u32[]{:S(2)}) %collective-permute-start.4) | collective-permute-done | bytes 544 | tf_op jit(solution)/shard_map/ppermute | solution.py:411
  34.6 23.5 %all_to_all.5 = f32[32,1,128]{2,1,0:T(1,128)S(1)} all-to-all(f32[32,1,128]{2,1,0:T(1,128)S(1)} %broadcast_in_dim.9), channel_id=1, replica_groups={{32,34,36,38,40,42,44,46,48,50,52,54,56,58,60,62,0,2,4,6,8,10,12,14,16,..., dimensions={0} | all-to-all | bytes 32768 | tf_op jit(solution)/shard_map/all_to_all | solution.py:444
  58.1 1.1 %finish.1 = (f32[32,3,128]{2,1,0:T(4,128)}, f32[32,3,128]{2,1,0:T(4,128)}) custom-call(f32[15,32,128]{2,1,0:T(8,128)S(1)} %get-tuple-element.10.basis_ref, f32[4,8,128]{2,1,0:T(8,128)S(1)} %bitcast.21), custom_call_target="tpu_custom_call" | custom-call | tf_op jit(solution)/shard_map/finish/pallas_call | solution.py:453
  (2 shorter events, 0.0 us)
Async XLA Ops:
  1.7 28.1 %collective-permute-start.2 = (f32[10,32,128]{2,1,0:T(8,128)S(1)}, f32[10,32,128]{2,1,0:T(8,128)S(1)}, u32[]{:S(2)}, u32[]{:S(2)}) collective-permute-start(f32[10,32,128]{2,1,0:T(8,128)S(1)} %pack.1.own_ref), channel_id=1, source_target_pairs={{0,1},{1,0},{2,3},{3,2},{4,5},{5,4},{6,7},{7,6},{8,9},{9,8},{10,11... | collective-permute-start | bytes 491528 | tf_op jit(solution)/shard_map/ppermute | solution.py:411
  22.3 7.5 %collective-permute-start.1 = (f32[10,32,128]{2,1,0:T(8,128)S(1)}, f32[10,32,128]{2,1,0:T(8,128)S(1)}, u32[]{:S(2)}, u32[]{:S(2)}) collective-permute-start(f32[10,32,128]{2,1,0:T(8,128)S(1)} %pack.1.own_ref), channel_id=1, source_target_pairs={{0,63},{1,2},{2,1},{3,4},{4,3},{5,6},{6,5},{7,8},{8,7},{9,10},{10,... | collective-permute-start | bytes 491528 | tf_op jit(solution)/shard_map/ppermute | solution.py:411
  22.5 7.3 %collective-permute-start = (f32[12,16,128]{2,1,0:T(8,128)S(1)}, f32[12,16,128]{2,1,0:T(8,128)S(1)}, u32[]{:S(2)}, u32[]{:S(2)}) collective-permute-start(f32[12,16,128]{2,1,0:T(8,128)S(1)} %get-tuple-element.8), channel_id=1, source_target_pairs={{0,2},{1,3},{2,4},{3,5},{4,6},{5,7},{6,8},{7,9},{8,10},{9,11},{10,... | collective-permute-start | bytes 294920 | tf_op jit(solution)/shard_map/ppermute | solution.py:411
  22.6 6.0 %collective-permute-start.3 = (f32[10,16,128]{2,1,0:T(8,128)S(1)}, f32[10,16,128]{2,1,0:T(8,128)S(1)}, u32[]{:S(2)}, u32[]{:S(2)}) collective-permute-start(f32[10,16,128]{2,1,0:T(8,128)S(1)} %get-tuple-element.9), channel_id=1, source_target_pairs={{0,62},{1,63},{2,0},{3,1},{4,2},{5,3},{6,4},{7,5},{8,6},{9,7},{10,... | collective-permute-start | bytes 245768 | tf_op jit(solution)/shard_map/ppermute | solution.py:411
  31.0 3.6 %collective-permute-start.4 = (f32[1,128]{1,0:T(1,128)S(1)}, f32[1,128]{1,0:T(1,128)S(1)}, u32[]{:S(2)}, u32[]{:S(2)}) collective-permute-start(f32[1,128]{1,0:T(1,128)S(1)} %get-tuple-element.11), channel_id=1, source_target_pairs={{0,1},{1,0},{2,3},{3,2},{4,5},{5,4},{6,7},{7,6},{8,9},{9,8},{10,11... | collective-permute-start | bytes 1544 | tf_op jit(solution)/shard_map/ppermute | solution.py:411

commit v6 on v5

--- a/solution.py
+++ b/solution.py
@@ -13,18 +13,25 @@
 
 CENTER = 5.7
 RADIUS = 2.3
+STILL = (DIAGONAL_SHIFT - CENTER) / RADIUS
 ORIGIN = -CENTER / RADIUS
 MOMENTS = 2 * ITERS
-LOWEST, HIGHEST = -2.2, 4.6
 
 f32 = jnp.float32
 
 
-def second_kind(order):
-    below, value = 0.0, 1.0
+def first_kind(order, at):
+    below, value = at, 1.0
     for _ in range(order):
-        below, value = value, 2.0 * ORIGIN * value - below
+        below, value = value, 2.0 * at * value - below
     return value
+
+
+def quotient(order, at):
+    second = [1.0, 2.0 * at]
+    while len(second) < order:
+        second.append(2.0 * at * second[-1] - second[-2])
+    return [(1.0 if i == 0 else 2.0) * second[order - 1 - i] for i in range(order)]
 
 
 def pack_kernel(first_ref, pos_hbm, rad_hbm, nb_hbm, rhs_hbm, out_ref, *scratch):
@@ -233,18 +240,18 @@
     kept = [cut(vector, depth, depth + rows)]
     push = fluxes(bonds, vector, lane, 0, total)
     lo, hi = 0, total
-    before, now = vector, []
+    before, now = None, []
     for c in range(3):
-        given = jnp.concatenate(
-            [ll_ref[7 + c], jnp.zeros((total - 2 * LY, LZ), f32), rr_ref[7 + c]], axis=0
-        )
-        image = f32(2.0 * (DIAGONAL_SHIFT - CENTER) / RADIUS) * vector[c]
-        now.append(f32(0.5) * (image + push[c] + given))
+        given = [ll_ref[7 + c], jnp.zeros((total - 2 * LY, LZ), f32), rr_ref[7 + c]]
+        now.append(push[c] + jnp.concatenate(given, axis=0))
     kept.append(cut(now, depth, depth + rows))
-    for _ in range(1, ITERS):
+    for k in range(1, ITERS):
         image = operate(now, lo, hi)
         m = hi - lo - 2 * LY
-        after = [x - p for x, p in zip(image, cut(before, LY, LY + m))]
+        if k == 1:
+            after = [f32(0.5) * x for x in image]
+        else:
+            after = [x - p for x, p in zip(image, cut(before, LY, LY + m))]
         before, now = cut(now, LY, LY + m), after
         lo, hi = lo + LY, hi - LY
         kept.append(cut(now, depth - lo, depth - lo + rows))
@@ -276,58 +283,50 @@
 
 
 def coefficients(products):
-    m = list(products[:2])
-    for k in range(2, MOMENTS):
-        m.append(2.0 * products[k] - m[k % 2])
-    zero = jnp.zeros_like(m[0])
-    one = jnp.ones_like(m[0])
-    s_before, s = [zero] * MOMENTS, m
-    alpha, beta = s[1] / s[0], None
-    ratio = alpha
-    c_before, c = [zero] * (ITERS + 1), [one] + [zero] * ITERS
-    p_before, p = zero, one
-    floor = s[0] * f32(1e-12)
-    for k in range(ITERS):
-        alpha = jnp.clip(alpha, LOWEST, HIGHEST)
-        nc = [zero] * (ITERS + 1)
-        for l in range(k + 1):
-            if l == 0:
-                nc[1] = nc[1] + c[0]
-            else:
-                nc[l - 1] = nc[l - 1] + 0.5 * c[l]
-                nc[l + 1] = nc[l + 1] + 0.5 * c[l]
-        for l in range(k + 1):
-            nc[l] = nc[l] - alpha * c[l]
-            if beta is not None and l < k:
-                nc[l] = nc[l] - beta * c_before[l]
-        np_ = (ORIGIN - alpha) * p
-        if beta is not None:
-            np_ = np_ - beta * p_before
-        if k + 1 < ITERS:
-            ns = [zero] * MOMENTS
-            for l in range(k + 1, MOMENTS - k - 1):
-                ns[l] = 0.5 * (s[l + 1] + s[abs(l - 1)]) - alpha * s[l]
-                if beta is not None:
-                    ns[l] = ns[l] - beta * s_before[l]
-            q = k + 1
-            den = jnp.maximum(ns[q], floor)
-            factor = 1.0 if q == 1 else 0.5
-            next_beta = factor * den / jnp.maximum(s[q - 1], floor)
-            new_ratio = ns[q + 1] / den * 0.5
-            alpha = new_ratio - ratio
-            ratio = new_ratio
-            s_before, s = s, ns
-            beta = next_beta
-        c_before, c = c, nc
-        p_before, p = p, np_
-    scale = 1.0 / p
-    res = [x * scale for x in c]
-    sol = []
+    size = ITERS + 1
+    zero = jnp.zeros_like(products[0])
+    nu = list(products[2:4])
+    for k in range(2, MOMENTS - 2):
+        nu.append(2.0 * products[2 + k] - nu[k % 2])
+    gram = [[None] * size for _ in range(size)]
+    gram[0][0] = products[0]
+    for k in range(1, size):
+        value = products[1] * f32(first_kind(k - 1, STILL))
+        for i, q in enumerate(quotient(k - 1, STILL) if k > 1 else ()):
+            value = value + nu[i] * f32(0.5 * q)
+        gram[0][k] = value
+    for i in range(1, ITERS):
+        for j in range(i, size):
+            gram[i][j] = 0.5 * (nu[i + j - 2] + nu[j - i])
+    scale = [gram[i][i] * f32(1e-8) for i in range(ITERS)]
+    lower = [[None] * ITERS for _ in range(size)]
     for i in range(ITERS):
-        total = zero
-        for j in range(i + 1, ITERS + 1):
-            total = total + res[j] * f32(second_kind(j - 1 - i))
-        sol.append(total * f32((-1.0 if i == 0 else -2.0) / RADIUS))
+        pivot = gram[i][i]
+        inverse = 1.0 / pivot
+        if i:
+            inverse = jnp.where(pivot > scale[i], inverse, zero)
+        for j in range(i + 1, size):
+            lower[j][i] = gram[i][j] * inverse
+        for k in range(i + 1, ITERS):
+            for j in range(k, size):
+                gram[k][j] = gram[k][j] - lower[k][i] * gram[i][j]
+    res = [None] * ITERS + [zero + 1.0]
+    for i in reversed(range(ITERS)):
+        value = lower[ITERS][i]
+        for j in range(i + 1, ITERS):
+            value = value + lower[j][i] * res[j]
+        res[i] = -value
+    at_origin = res[0]
+    for k in range(1, size):
+        weight = -2.0 * DIAGONAL_SHIFT / RADIUS * first_kind(k - 1, ORIGIN)
+        at_origin = at_origin + res[k] * f32(weight)
+    unit = 1.0 / at_origin
+    res = [x * unit for x in res]
+    sol = [zero] * ITERS
+    for j in range(1, size):
+        sol[0] = sol[0] - res[j] * f32(2.0 / RADIUS * first_kind(j - 1, ORIGIN))
+        for i, q in enumerate(quotient(j - 1, ORIGIN) if j > 1 else ()):
+            sol[i + 1] = sol[i + 1] - res[j] * f32(q / RADIUS)
     return res, sol
 
 

time: 59.7 us -> 59.7 us (level)
  no operation moved by 1% of the time
where the time goes in v6:
time: 59.7 us; the launch traced here: 59.2 us
  starting transfers between devices  27.3 us (46%)
  blocking collectives  23.5 us (39%)
  waiting for transfers between devices  4.12 us (7%)
  Pallas kernels  3.55 us (6%)
  between operations  0.67 us (1%)
    ppermute x5, starting transfers between devices, moved(): lax.ppermute(array, 'gx', [(i, to(i) % devices) for i in range(devices)])  27.3 us
    all_to_all x1, blocking collectives, on_device(): lax.all_to_all(jnp.broadcast_to(sums[None], (chips, 1, LZ)), 'gx', split_...  23.5 us
    ppermute x5, waiting for transfers between devices, moved(): lax.ppermute(array, 'gx', [(i, to(i) % devices) for i in range(devices)])  4.12 us
  transfers between devices with their start and end apart: 5, of which 3 were waited for; matrix products, arithmetic and copies ran while one was open for 0% of the time, Pallas kernels for 0%

profile of v6, /device:TPU:37, one launch (start us, length us, event | category | flops | bytes accessed | tf_op | source)
XLA Modules:
  0.0 59.2 jit_solution(11595845090183621435)
XLA Ops:
  0.6 1.1 %pack.1.own_ref = f32[10,32,128]{2,1,0:T(8,128)S(1)} custom-call(s32[1]{0:T(128)} %bitcast.1.first_ref, f32[32,3,128]{2,1,0:T(4,128)} %bitcast.23, f32[32,128]{1,0:T(8,128)} %bitcast.25, s32[32,6,128]{2,1,0:T(8,128)} %bitcast.22, f32[32,3,128]{2,1,0:T(4,128)} %bitcast.24), custom_call_target="tpu_custom_call" | custom-call | tf_op jit(solution)/shard_map/pack/pallas_call | solution.py:387
  1.7 20.5 %collective-permute-start.2 = (f32[10,32,128]{2,1,0:T(8,128)S(1)}, f32[10,32,128]{2,1,0:T(8,128)S(1)}, u32[]{:S(2)}, u32[]{:S(2)}) collective-permute-start(f32[10,32,128]{2,1,0:T(8,128)S(1)} %pack.1.own_ref), channel_id=1, source_target_pairs={{0,1},{1,0},{2,3},{3,2},{4,5},{5,4},{6,7},{7,6},{8,9},{9,8},{10,11... | collective-permute-start | bytes 491528 | tf_op jit(solution)/shard_map/ppermute | solution.py:410
  22.3 0.0 collective-permute-start.1
  22.3 0.2 edge.1
  22.5 0.1 collective-permute-start
  22.6 3.9 %collective-permute-start.3 = (f32[10,16,128]{2,1,0:T(8,128)S(1)}, f32[10,16,128]{2,1,0:T(8,128)S(1)}, u32[]{:S(2)}, u32[]{:S(2)}) collective-permute-start(f32[10,16,128]{2,1,0:T(8,128)S(1)} %get-tuple-element.9), channel_id=1, source_target_pairs={{0,62},{1,63},{2,0},{3,1},{4,2},{5,3},{6,4},{7,5},{8,6},{9,7},{10,... | collective-permute-start | bytes 245768 | tf_op jit(solution)/shard_map/ppermute | solution.py:410
  26.5 2.1 %collective-permute-done.3.rr_ref = f32[10,16,128]{2,1,0:T(8,128)S(1)} collective-permute-done((f32[10,16,128]{2,1,0:T(8,128)S(1)}, f32[10,16,128]{2,1,0:T(8,128)S(1)}, u32[]{:S(2)}, u32[]{:S(2)}) %collective-permute-start.3) | collective-permute-done | bytes 81952 | tf_op jit(solution)/shard_map/ppermute | solution.py:410
  28.6 1.2 %collective-permute-done.ll_ref = f32[12,16,128]{2,1,0:T(8,128)S(1)} collective-permute-done((f32[12,16,128]{2,1,0:T(8,128)S(1)}, f32[12,16,128]{2,1,0:T(8,128)S(1)}, u32[]{:S(2)}, u32[]{:S(2)}) %collective-permute-start) | collective-permute-done | bytes 98336 | tf_op jit(solution)/shard_map/ppermute | solution.py:410
  29.8 0.0 collective-permute-done.2.mate_ref
  29.8 0.0 collective-permute-done.1.far_ref
  29.8 1.1 %krylov.1 = (f32[15,32,128]{2,1,0:T(8,128)S(1)}, f32[1,128]{1,0:T(1,128)S(1)}) custom-call(s32[1]{0:T(128)} %bitcast.odd_ref, f32[12,16,128]{2,1,0:T(8,128)S(1)} %collective-permute-done.ll_ref, f32[10,32,128]{2,1,0:T(8,128)S(1)} %collective-permute-done.1.far_ref, f32[10,32,128]{2,1,0:T(8,128)S(1)} %pack.1.own_ref, ...), custom_call_target="tpu_custom_call" | custom-call | tf_op jit(solution)/shard_map/krylov/pallas_call | solution.py:428
  30.9 2.8 %collective-permute-start.4 = (f32[1,128]{1,0:T(1,128)S(1)}, f32[1,128]{1,0:T(1,128)S(1)}, u32[]{:S(2)}, u32[]{:S(2)}) collective-permute-start(f32[1,128]{1,0:T(1,128)S(1)} %get-tuple-element.11), channel_id=1, source_target_pairs={{0,1},{1,0},{2,3},{3,2},{4,5},{5,4},{6,7},{7,6},{8,9},{9,8},{10,11... | collective-permute-start | bytes 1544 | tf_op jit(solution)/shard_map/ppermute | solution.py:410
  33.7 0.8 %collective-permute-done.4 = f32[1,128]{1,0:T(1,128)S(1)} collective-permute-done((f32[1,128]{1,0:T(1,128)S(1)}, f32[1,128]{1,0:T(1,128)S(1)}, u32[]{:S(2)}, u32[]{:S(2)}) %collective-permute-start.4) | collective-permute-done | bytes 544 | tf_op jit(solution)/shard_map/ppermute | solution.py:410
  34.6 23.5 %all_to_all.5 = f32[32,1,128]{2,1,0:T(1,128)S(1)} all-to-all(f32[32,1,128]{2,1,0:T(1,128)S(1)} %broadcast_in_dim.9), channel_id=1, replica_groups={{32,34,36,38,40,42,44,46,48,50,52,54,56,58,60,62,0,2,4,6,8,10,12,14,16,..., dimensions={0} | all-to-all | bytes 32768 | tf_op jit(solution)/shard_map/all_to_all | solution.py:443
  58.1 1.1 %finish.1 = (f32[32,3,128]{2,1,0:T(4,128)}, f32[32,3,128]{2,1,0:T(4,128)}) custom-call(f32[15,32,128]{2,1,0:T(8,128)S(1)} %get-tuple-element.10.basis_ref, f32[4,8,128]{2,1,0:T(8,128)S(1)} %bitcast.21), custom_call_target="tpu_custom_call" | custom-call | tf_op jit(solution)/shard_map/finish/pallas_call | solution.py:452
  (2 shorter events, 0.0 us)
Async XLA Ops:
  1.7 28.1 %collective-permute-start.2 = (f32[10,32,128]{2,1,0:T(8,128)S(1)}, f32[10,32,128]{2,1,0:T(8,128)S(1)}, u32[]{:S(2)}, u32[]{:S(2)}) collective-permute-start(f32[10,32,128]{2,1,0:T(8,128)S(1)} %pack.1.own_ref), channel_id=1, source_target_pairs={{0,1},{1,0},{2,3},{3,2},{4,5},{5,4},{6,7},{7,6},{8,9},{9,8},{10,11... | collective-permute-start | bytes 491528 | tf_op jit(solution)/shard_map/ppermute | solution.py:410
  22.3 7.5 %collective-permute-start.1 = (f32[10,32,128]{2,1,0:T(8,128)S(1)}, f32[10,32,128]{2,1,0:T(8,128)S(1)}, u32[]{:S(2)}, u32[]{:S(2)}) collective-permute-start(f32[10,32,128]{2,1,0:T(8,128)S(1)} %pack.1.own_ref), channel_id=1, source_target_pairs={{0,63},{1,2},{2,1},{3,4},{4,3},{5,6},{6,5},{7,8},{8,7},{9,10},{10,... | collective-permute-start | bytes 491528 | tf_op jit(solution)/shard_map/ppermute | solution.py:410
  22.5 7.3 %collective-permute-start = (f32[12,16,128]{2,1,0:T(8,128)S(1)}, f32[12,16,128]{2,1,0:T(8,128)S(1)}, u32[]{:S(2)}, u32[]{:S(2)}) collective-permute-start(f32[12,16,128]{2,1,0:T(8,128)S(1)} %get-tuple-element.8), channel_id=1, source_target_pairs={{0,2},{1,3},{2,4},{3,5},{4,6},{5,7},{6,8},{7,9},{8,10},{9,11},{10,... | collective-permute-start | bytes 294920 | tf_op jit(solution)/shard_map/ppermute | solution.py:410
  22.6 6.0 %collective-permute-start.3 = (f32[10,16,128]{2,1,0:T(8,128)S(1)}, f32[10,16,128]{2,1,0:T(8,128)S(1)}, u32[]{:S(2)}, u32[]{:S(2)}) collective-permute-start(f32[10,16,128]{2,1,0:T(8,128)S(1)} %get-tuple-element.9), channel_id=1, source_target_pairs={{0,62},{1,63},{2,0},{3,1},{4,2},{5,3},{6,4},{7,5},{8,6},{9,7},{10,... | collective-permute-start | bytes 245768 | tf_op jit(solution)/shard_map/ppermute | solution.py:410
  30.9 3.6 %collective-permute-start.4 = (f32[1,128]{1,0:T(1,128)S(1)}, f32[1,128]{1,0:T(1,128)S(1)}, u32[]{:S(2)}, u32[]{:S(2)}) collective-permute-start(f32[1,128]{1,0:T(1,128)S(1)} %get-tuple-element.11), channel_id=1, source_target_pairs={{0,1},{1,0},{2,3},{3,2},{4,5},{5,4},{6,7},{7,6},{8,9},{9,8},{10,11... | collective-permute-start | bytes 1544 | tf_op jit(solution)/shard_map/ppermute | solution.py:410

commit v7 on v6

--- a/solution.py
+++ b/solution.py
@@ -34,7 +34,9 @@
     return [(1.0 if i == 0 else 2.0) * second[order - 1 - i] for i in range(order)]
 
 
-def pack_kernel(first_ref, pos_hbm, rad_hbm, nb_hbm, rhs_hbm, out_ref, *scratch):
+def pack_kernel(
+    first_ref, pos_hbm, rad_hbm, nb_hbm, rhs_hbm, out_ref, low_ref, high_ref, *scratch
+):
     pos_ref, rad_ref, nb_ref, rhs_ref, sems = scratch
     moves = [
         pltpu.make_async_copy(src, dst, sems.at[k])
@@ -55,21 +57,23 @@
         lax.broadcasted_iota(jnp.int32, shape, 0) * LZ
         + lax.broadcasted_iota(jnp.int32, shape, 1)
     )
-    for move in moves:
+    for move in moves[1:]:
         move.wait()
+    for c in range(3):
+        out_ref[c] = pos_ref[:, c, :]
+        out_ref[7 + c] = rhs_ref[:, c, :]
+    out_ref[3] = rad_ref[...]
+    moves[0].wait()
     slots = [nb_ref[:, s, :] - ids for s in range(nb_ref.shape[1])]
     for b, shift in enumerate((LY * LZ, LZ, 1)):
         hit = slots[0] == shift
         for other in slots[1:]:
             hit = hit | (other == shift)
         out_ref[4 + b] = jnp.where(hit, f32(1.0), f32(0.0))
-    for c in range(3):
-        out_ref[c] = pos_ref[:, c, :]
-        out_ref[7 + c] = rhs_ref[:, c, :]
-    out_ref[3] = rad_ref[...]
-
-
-def edge_kernel(own_ref, low_ref, high_ref):
+    write_edges(out_ref, low_ref, high_ref)
+
+
+def write_edges(own_ref, low_ref, high_ref):
     rows = own_ref.shape[1]
     row, lane = coordinates(rows)
     geom = [own_ref[c] for c in range(4)]
@@ -118,18 +122,15 @@
 
 
 def bond(mask, delta, contact, allowed=None):
+    if allowed is not None:
+        mask = jnp.where(allowed, mask, f32(0.0))
     squared = delta[0] * delta[0] + delta[1] * delta[1] + delta[2] * delta[2]
-    live = mask > 0.5
-    if allowed is not None:
-        live = live & allowed
-    squared = jnp.where(live, squared, f32(1.0))
     shrink = lax.rsqrt(squared)
     inverse = 1.0 / (contact * (squared * shrink))
     scaled = inverse * f32(2.0 / RADIUS)
-    tension = (squared * inverse - 1.0) * scaled
-    weight = (scaled * lax.rsqrt(scaled)) * shrink
-    tension = jnp.where(live, tension, f32(0.0))
-    weight = jnp.where(live, weight, f32(0.0))
+    present = scaled * mask
+    tension = (squared * inverse - 1.0) * present
+    weight = (present * lax.rsqrt(scaled)) * shrink
     return tension, [d * weight for d in delta]
 
 
@@ -210,18 +211,18 @@
 
     none = jnp.zeros((LY, LZ), f32)
     pad = jnp.zeros((LY - half, LZ), f32)
-    rim = row == LY - 1
-    past = row >= LY
+    rim = row[:half] == half - 1
+    corner = rim & (lane[:half] == LZ - 1)
+    low_y = jnp.where(rim, ll_ref[11, :half, :], f32(0.0))
+    low_z = jnp.where(corner, ll_ref[11, half:, :], f32(0.0))
     geom = [ext(c, ll_ref[c], rr_ref[c]) for c in range(4)]
     vector = [ext(7 + c, ll_ref[4 + c], rr_ref[4 + c]) for c in range(3)]
     masks = [
         ext(4, ll_ref[10], none),
-        ext(5, jnp.concatenate([pad, ll_ref[11, :half, :]], axis=0), none),
-        ext(6, jnp.concatenate([pad, ll_ref[11, half:, :]], axis=0), none),
+        ext(5, jnp.concatenate([pad, low_y], axis=0), none),
+        ext(6, jnp.concatenate([pad, low_z], axis=0), none),
     ]
-    bonds = all_bonds(
-        geom, masks, lane, (None, past | rim, past | (rim & (lane == LZ - 1)))
-    )
+    bonds = all_bonds(geom, masks, lane)
 
     def operate(v, lo, hi):
         n = hi - lo
@@ -384,11 +385,15 @@
     smem = pl.BlockSpec(memory_space=pltpu.SMEM)
     hbm = pl.BlockSpec(memory_space=pltpu.HBM)
 
-    packed = pl.pallas_call(
+    packed, low, high = pl.pallas_call(
         pack_kernel,
-        out_shape=jax.ShapeDtypeStruct((10, rows, LZ), f32),
+        out_shape=(
+            jax.ShapeDtypeStruct((10, rows, LZ), f32),
+            jax.ShapeDtypeStruct((10, LY, LZ), f32),
+            jax.ShapeDtypeStruct((12, LY, LZ), f32),
+        ),
         in_specs=[smem, hbm, hbm, hbm, hbm],
-        out_specs=vmem,
+        out_specs=(vmem,) * 3,
         scratch_shapes=[
             pltpu.VMEM((rows, 3, LZ), f32),
             pltpu.VMEM((rows, LZ), f32),
@@ -409,17 +414,6 @@
     def moved(array, to):
         return lax.ppermute(array, "gx", [(i, to(i) % devices) for i in range(devices)])
 
-    low, high = pl.pallas_call(
-        edge_kernel,
-        out_shape=(
-            jax.ShapeDtypeStruct((10, LY, LZ), f32),
-            jax.ShapeDtypeStruct((12, LY, LZ), f32),
-        ),
-        in_specs=[vmem],
-        out_specs=(vmem, vmem),
-        compiler_params=pltpu.CompilerParams(vmem_limit_bytes=4 << 20),
-        name="edge",
-    )(packed)
     across = moved(packed, lambda i: i + 1 if i % 2 else i - 1)
     far_left = moved(high, lambda i: i + 2)
     far_right = moved(low, lambda i: i - 2)

time: 59.7 us -> 59.5 us (level)
    pallas_call x2 -> x1, Pallas kernels: 1.28 us -> 1.21 us  [on_device(): pl.pallas_call(pack_kernel, out_shape=(jax.ShapeDtypeStruct((10, rows, LZ...]
where the time goes in v7:
time: 59.5 us; the launch traced here: 59 us
  starting transfers between devices  26.8 us (45%)
  blocking collectives  23.5 us (39%)
  waiting for transfers between devices  4.58 us (8%)
  Pallas kernels  3.47 us (6%)
  between operations  0.65 us (1%)
    ppermute x5, starting transfers between devices, moved(): lax.ppermute(array, 'gx', [(i, to(i) % devices) for i in range(devices)])  26.8 us
    all_to_all x1, blocking collectives, on_device(): lax.all_to_all(jnp.broadcast_to(sums[None], (chips, 1, LZ)), 'gx', split_...  23.5 us
    ppermute x5, waiting for transfers between devices, moved(): lax.ppermute(array, 'gx', [(i, to(i) % devices) for i in range(devices)])  4.58 us
    pallas_call x1, Pallas kernels, on_device(): pl.pallas_call(pack_kernel, out_shape=(jax.ShapeDtypeStruct((10, rows, LZ...  1.21 us
  transfers between devices with their start and end apart: 5, of which 3 were waited for; matrix products, arithmetic and copies ran while one was open for 0% of the time, Pallas kernels for 0%

profile of v7, /device:TPU:37, one launch (start us, length us, event | category | flops | bytes accessed | tf_op | source)
XLA Modules:
  0.0 59.0 jit_solution(10123149561261715129)
XLA Ops:
  0.6 1.2 %pack.1 = (f32[10,32,128]{2,1,0:T(8,128)S(1)}, f32[10,16,128]{2,1,0:T(8,128)S(1)}, f32[12,16,128]{2,1,0:T(8,128)S(1)}) custom-call(s32[1]{0:T(128)} %bitcast.1.first_ref, f32[32,3,128]{2,1,0:T(4,128)} %bitcast.23, f32[32,128]{1,0:T(8,128)} %bitcast.25, s32[32,6,128]{2,1,0:T(8,128)} %bitcast.22, f32[32,3,128]{2,1,0:T(4,128)} %bitcast.24), custom_call_target="tpu_custom_call" | custom-call | tf_op jit(solution)/shard_map/pack/pallas_call | solution.py:388
  1.8 20.5 %collective-permute-start.2 = (f32[10,32,128]{2,1,0:T(8,128)S(1)}, f32[10,32,128]{2,1,0:T(8,128)S(1)}, u32[]{:S(2)}, u32[]{:S(2)}) collective-permute-start(f32[10,32,128]{2,1,0:T(8,128)S(1)} %get-tuple-element.10.own_ref), channel_id=1, source_target_pairs={{0,1},{1,0},{2,3},{3,2},{4,5},{5,4},{6,7},{7,6},{8,9},{9,8},{10,11... | collective-permute-start | bytes 491528 | tf_op jit(solution)/shard_map/ppermute | solution.py:415
  22.4 0.0 collective-permute-start.1
  22.4 0.0 collective-permute-start
  22.4 3.8 %collective-permute-start.3 = (f32[10,16,128]{2,1,0:T(8,128)S(1)}, f32[10,16,128]{2,1,0:T(8,128)S(1)}, u32[]{:S(2)}, u32[]{:S(2)}) collective-permute-start(f32[10,16,128]{2,1,0:T(8,128)S(1)} %get-tuple-element.11), channel_id=1, source_target_pairs={{0,62},{1,63},{2,0},{3,1},{4,2},{5,3},{6,4},{7,5},{8,6},{9,7},{10,... | collective-permute-start | bytes 245768 | tf_op jit(solution)/shard_map/ppermute | solution.py:415
  26.2 1.7 %collective-permute-done.3.rr_ref = f32[10,16,128]{2,1,0:T(8,128)S(1)} collective-permute-done((f32[10,16,128]{2,1,0:T(8,128)S(1)}, f32[10,16,128]{2,1,0:T(8,128)S(1)}, u32[]{:S(2)}, u32[]{:S(2)}) %collective-permute-start.3) | collective-permute-done | bytes 81952 | tf_op jit(solution)/shard_map/ppermute | solution.py:415
  27.9 2.1 %collective-permute-done.ll_ref = f32[12,16,128]{2,1,0:T(8,128)S(1)} collective-permute-done((f32[12,16,128]{2,1,0:T(8,128)S(1)}, f32[12,16,128]{2,1,0:T(8,128)S(1)}, u32[]{:S(2)}, u32[]{:S(2)}) %collective-permute-start) | collective-permute-done | bytes 98336 | tf_op jit(solution)/shard_map/ppermute | solution.py:415
  29.9 0.0 collective-permute-done.2.mate_ref
  29.9 0.0 collective-permute-done.1.far_ref
  29.9 1.1 %krylov.1 = (f32[15,32,128]{2,1,0:T(8,128)S(1)}, f32[1,128]{1,0:T(1,128)S(1)}) custom-call(s32[1]{0:T(128)} %bitcast.odd_ref, f32[12,16,128]{2,1,0:T(8,128)S(1)} %collective-permute-done.ll_ref, f32[10,32,128]{2,1,0:T(8,128)S(1)} %collective-permute-done.1.far_ref, f32[10,32,128]{2,1,0:T(8,128)S(1)} %get-tuple-element.10.own_ref, ...), custom_call_target="tpu_custom_call" | custom-call | tf_op jit(solution)/shard_map/krylov/pallas_call | solution.py:422
  31.1 2.5 %collective-permute-start.4 = (f32[1,128]{1,0:T(1,128)S(1)}, f32[1,128]{1,0:T(1,128)S(1)}, u32[]{:S(2)}, u32[]{:S(2)}) collective-permute-start(f32[1,128]{1,0:T(1,128)S(1)} %get-tuple-element.13), channel_id=1, source_target_pairs={{0,1},{1,0},{2,3},{3,2},{4,5},{5,4},{6,7},{7,6},{8,9},{9,8},{10,11... | collective-permute-start | bytes 1544 | tf_op jit(solution)/shard_map/ppermute | solution.py:415
  33.5 0.8 %collective-permute-done.4 = f32[1,128]{1,0:T(1,128)S(1)} collective-permute-done((f32[1,128]{1,0:T(1,128)S(1)}, f32[1,128]{1,0:T(1,128)S(1)}, u32[]{:S(2)}, u32[]{:S(2)}) %collective-permute-start.4) | collective-permute-done | bytes 544 | tf_op jit(solution)/shard_map/ppermute | solution.py:415
  34.4 23.5 %all_to_all.5 = f32[32,1,128]{2,1,0:T(1,128)S(1)} all-to-all(f32[32,1,128]{2,1,0:T(1,128)S(1)} %broadcast_in_dim.9), channel_id=1, replica_groups={{32,34,36,38,40,42,44,46,48,50,52,54,56,58,60,62,0,2,4,6,8,10,12,14,16,..., dimensions={0} | all-to-all | bytes 32768 | tf_op jit(solution)/shard_map/all_to_all | solution.py:437
  57.9 1.1 %finish.1 = (f32[32,3,128]{2,1,0:T(4,128)}, f32[32,3,128]{2,1,0:T(4,128)}) custom-call(f32[15,32,128]{2,1,0:T(8,128)S(1)} %get-tuple-element.12.basis_ref, f32[4,8,128]{2,1,0:T(8,128)S(1)} %bitcast.21), custom_call_target="tpu_custom_call" | custom-call | tf_op jit(solution)/shard_map/finish/pallas_call | solution.py:446
  (2 shorter events, 0.0 us)
Async XLA Ops:
  1.8 28.1 %collective-permute-start.2 = (f32[10,32,128]{2,1,0:T(8,128)S(1)}, f32[10,32,128]{2,1,0:T(8,128)S(1)}, u32[]{:S(2)}, u32[]{:S(2)}) collective-permute-start(f32[10,32,128]{2,1,0:T(8,128)S(1)} %get-tuple-element.10.own_ref), channel_id=1, source_target_pairs={{0,1},{1,0},{2,3},{3,2},{4,5},{5,4},{6,7},{7,6},{8,9},{9,8},{10,11... | collective-permute-start | bytes 491528 | tf_op jit(solution)/shard_map/ppermute | solution.py:415
  22.4 7.5 %collective-permute-start.1 = (f32[10,32,128]{2,1,0:T(8,128)S(1)}, f32[10,32,128]{2,1,0:T(8,128)S(1)}, u32[]{:S(2)}, u32[]{:S(2)}) collective-permute-start(f32[10,32,128]{2,1,0:T(8,128)S(1)} %get-tuple-element.10.own_ref), channel_id=1, source_target_pairs={{0,63},{1,2},{2,1},{3,4},{4,3},{5,6},{6,5},{7,8},{8,7},{9,10},{10,... | collective-permute-start | bytes 491528 | tf_op jit(solution)/shard_map/ppermute | solution.py:415
  22.4 7.5 %collective-permute-start = (f32[12,16,128]{2,1,0:T(8,128)S(1)}, f32[12,16,128]{2,1,0:T(8,128)S(1)}, u32[]{:S(2)}, u32[]{:S(2)}) collective-permute-start(f32[12,16,128]{2,1,0:T(8,128)S(1)} %get-tuple-element.9), channel_id=1, source_target_pairs={{0,2},{1,3},{2,4},{3,5},{4,6},{5,7},{6,8},{7,9},{8,10},{9,11},{10,... | collective-permute-start | bytes 294920 | tf_op jit(solution)/shard_map/ppermute | solution.py:415
  22.4 5.5 %collective-permute-start.3 = (f32[10,16,128]{2,1,0:T(8,128)S(1)}, f32[10,16,128]{2,1,0:T(8,128)S(1)}, u32[]{:S(2)}, u32[]{:S(2)}) collective-permute-start(f32[10,16,128]{2,1,0:T(8,128)S(1)} %get-tuple-element.11), channel_id=1, source_target_pairs={{0,62},{1,63},{2,0},{3,1},{4,2},{5,3},{6,4},{7,5},{8,6},{9,7},{10,... | collective-permute-start | bytes 245768 | tf_op jit(solution)/shard_map/ppermute | solution.py:415
  31.1 3.3 %collective-permute-start.4 = (f32[1,128]{1,0:T(1,128)S(1)}, f32[1,128]{1,0:T(1,128)S(1)}, u32[]{:S(2)}, u32[]{:S(2)}) collective-permute-start(f32[1,128]{1,0:T(1,128)S(1)} %get-tuple-element.13), channel_id=1, source_target_pairs={{0,1},{1,0},{2,3},{3,2},{4,5},{5,4},{6,7},{7,6},{8,9},{9,8},{10,11... | collective-permute-start | bytes 1544 | tf_op jit(solution)/shard_map/ppermute | solution.py:415

commit v8 on v7

--- a/solution.py
+++ b/solution.py
@@ -193,21 +193,15 @@
     return result
 
 
-def krylov_kernel(
-    odd_ref, ll_ref, far_ref, own_ref, mate_ref, rr_ref, basis_ref, sums_ref
-):
+def krylov_kernel(ll_ref, l_ref, own_ref, r_ref, rr_ref, basis_ref, sums_ref):
     rows = own_ref.shape[1]
-    odd = odd_ref[0] == 1
     depth = rows + LY
     total = rows + 2 * depth
     row, lane = coordinates(total)
     half = LY // 2
 
     def ext(c, low, high):
-        outer, mate = far_ref[c], mate_ref[c]
-        left = jnp.where(odd, mate, outer)
-        right = jnp.where(odd, outer, mate)
-        return jnp.concatenate([low, left, own_ref[c], right, high], axis=0)
+        return jnp.concatenate([low, l_ref[c], own_ref[c], r_ref[c], high], axis=0)
 
     none = jnp.zeros((LY, LZ), f32)
     pad = jnp.zeros((LY - half, LZ), f32)
@@ -378,9 +372,7 @@
     owned = positions.shape[1]
     rows = owned // LZ
     devices = lax.axis_size("gx")
-    place = lax.axis_index("gx").astype(jnp.int32)
-    first = (place * owned).reshape(1)
-    odd = (place % 2).reshape(1)
+    first = (lax.axis_index("gx") * owned).astype(jnp.int32).reshape(1)
     vmem = pl.BlockSpec(memory_space=pltpu.VMEM)
     smem = pl.BlockSpec(memory_space=pltpu.SMEM)
     hbm = pl.BlockSpec(memory_space=pltpu.HBM)
@@ -414,10 +406,10 @@
     def moved(array, to):
         return lax.ppermute(array, "gx", [(i, to(i) % devices) for i in range(devices)])
 
-    across = moved(packed, lambda i: i + 1 if i % 2 else i - 1)
+    left = moved(packed, lambda i: i + 1)
     far_left = moved(high, lambda i: i + 2)
     far_right = moved(low, lambda i: i - 2)
-    mate = moved(packed, lambda i: i ^ 1)
+    right = moved(packed, lambda i: i - 1)
 
     basis, sums = pl.pallas_call(
         krylov_kernel,
@@ -425,11 +417,11 @@
             jax.ShapeDtypeStruct((3 * (ITERS + 1), rows, LZ), f32),
             jax.ShapeDtypeStruct((1, LZ), f32),
         ),
-        in_specs=[smem] + [vmem] * 5,
+        in_specs=[vmem] * 5,
         out_specs=(vmem, vmem),
         compiler_params=pltpu.CompilerParams(vmem_limit_bytes=12 << 20),
         name="krylov",
-    )(odd, far_left, across, packed, mate, far_right)
+    )(far_left, left, packed, right, far_right)
 
     chips = devices // 2
     sums = sums + moved(sums, lambda i: i ^ 1)

time: 59.5 us -> 60.1 us (1.010)
  waiting for transfers between devices: 4.58 us -> 5.97 us
    ppermute x5, waiting for transfers between devices: 4.58 us -> 5.97 us  [moved(): lax.ppermute(array, 'gx', [(i, to(i) % devices) for i in range(devices)])]
where the time goes in v8:
time: 60.1 us; the launch traced here: 59.8 us
  starting transfers between devices  26.6 us (44%)
  blocking collectives  23.1 us (38%)
  waiting for transfers between devices  5.97 us (10%)
  Pallas kernels  3.45 us (6%)
  between operations  0.65 us (1%)
    ppermute x5, starting transfers between devices, moved(): lax.ppermute(array, 'gx', [(i, to(i) % devices) for i in range(devices)])  26.6 us
    all_to_all x1, blocking collectives, on_device(): lax.all_to_all(jnp.broadcast_to(sums[None], (chips, 1, LZ)), 'gx', split_...  23.1 us
    ppermute x5, waiting for transfers between devices, moved(): lax.ppermute(array, 'gx', [(i, to(i) % devices) for i in range(devices)])  5.97 us
    pallas_call x1, Pallas kernels, on_device(): pl.pallas_call(pack_kernel, out_shape=(jax.ShapeDtypeStruct((10, rows, LZ...  1.21 us
  transfers between devices with their start and end apart: 5, of which 3 were waited for; matrix products, arithmetic and copies ran while one was open for 0% of the time, Pallas kernels for 0%

profile of v8, /device:TPU:37, one launch (start us, length us, event | category | flops | bytes accessed | tf_op | source)
XLA Modules:
  0.0 59.8 jit_solution(15070426211616310472)
XLA Ops:
  0.6 1.2 %pack.1 = (f32[10,32,128]{2,1,0:T(8,128)S(1)}, f32[10,16,128]{2,1,0:T(8,128)S(1)}, f32[12,16,128]{2,1,0:T(8,128)S(1)}) custom-call(s32[1]{0:T(128)} %bitcast.first_ref, f32[32,3,128]{2,1,0:T(4,128)} %bitcast.22, f32[32,128]{1,0:T(8,128)} %bitcast.24, s32[32,6,128]{2,1,0:T(8,128)} %bitcast.21, f32[32,3,128]{2,1,0:T(4,128)} %bitcast.23), custom_call_target="tpu_custom_call" | custom-call | tf_op jit(solution)/shard_map/pack/pallas_call | solution.py:380
  1.8 20.5 %collective-permute-start.2 = (f32[10,32,128]{2,1,0:T(8,128)S(1)}, f32[10,32,128]{2,1,0:T(8,128)S(1)}, u32[]{:S(2)}, u32[]{:S(2)}) collective-permute-start(f32[10,32,128]{2,1,0:T(8,128)S(1)} %get-tuple-element.10.own_ref), channel_id=1, source_target_pairs={{0,63},{1,0},{2,1},{3,2},{4,3},{5,4},{6,5},{7,6},{8,7},{9,8},{10,9... | collective-permute-start | bytes 491528 | tf_op jit(solution)/shard_map/ppermute | solution.py:407
  22.3 0.0 collective-permute-start.1
  22.3 0.0 collective-permute-start
  22.3 6.1 %collective-permute-start.3 = (f32[10,16,128]{2,1,0:T(8,128)S(1)}, f32[10,16,128]{2,1,0:T(8,128)S(1)}, u32[]{:S(2)}, u32[]{:S(2)}) collective-permute-start(f32[10,16,128]{2,1,0:T(8,128)S(1)} %get-tuple-element.11), channel_id=1, source_target_pairs={{0,62},{1,63},{2,0},{3,1},{4,2},{5,3},{6,4},{7,5},{8,6},{9,7},{10,... | collective-permute-start | bytes 245768 | tf_op jit(solution)/shard_map/ppermute | solution.py:407
  28.4 1.5 %collective-permute-done.3.rr_ref = f32[10,16,128]{2,1,0:T(8,128)S(1)} collective-permute-done((f32[10,16,128]{2,1,0:T(8,128)S(1)}, f32[10,16,128]{2,1,0:T(8,128)S(1)}, u32[]{:S(2)}, u32[]{:S(2)}) %collective-permute-start.3) | collective-permute-done | bytes 81952 | tf_op jit(solution)/shard_map/ppermute | solution.py:407
  29.9 3.3 %collective-permute-done.ll_ref = f32[12,16,128]{2,1,0:T(8,128)S(1)} collective-permute-done((f32[12,16,128]{2,1,0:T(8,128)S(1)}, f32[12,16,128]{2,1,0:T(8,128)S(1)}, u32[]{:S(2)}, u32[]{:S(2)}) %collective-permute-start) | collective-permute-done | bytes 98336 | tf_op jit(solution)/shard_map/ppermute | solution.py:407
  33.2 0.0 collective-permute-done.2.r_ref
  33.2 0.0 collective-permute-done.1.l_ref
  33.2 1.1 %krylov.1 = (f32[15,32,128]{2,1,0:T(8,128)S(1)}, f32[1,128]{1,0:T(1,128)S(1)}) custom-call(f32[12,16,128]{2,1,0:T(8,128)S(1)} %collective-permute-done.ll_ref, f32[10,32,128]{2,1,0:T(8,128)S(1)} %collective-permute-done.1.l_ref, f32[10,32,128]{2,1,0:T(8,128)S(1)} %get-tuple-element.10.own_ref, f32[10,32,128]{2,1,0:T(8,128)S(1)} %collective-permute-done.2.r_ref, ...), custom_call_target="tpu_custom_call" | custom-call | tf_op jit(solution)/shard_map/krylov/pallas_call | solution.py:414
  34.4 0.0 collective-permute-start.4
  34.4 1.2 %collective-permute-done.4 = f32[1,128]{1,0:T(1,128)S(1)} collective-permute-done((f32[1,128]{1,0:T(1,128)S(1)}, f32[1,128]{1,0:T(1,128)S(1)}, u32[]{:S(2)}, u32[]{:S(2)}) %collective-permute-start.4) | collective-permute-done | bytes 544 | tf_op jit(solution)/shard_map/ppermute | solution.py:407
  35.5 23.1 %all_to_all.5 = f32[32,1,128]{2,1,0:T(1,128)S(1)} all-to-all(f32[32,1,128]{2,1,0:T(1,128)S(1)} %broadcast_in_dim.9), channel_id=1, replica_groups={{32,34,36,38,40,42,44,46,48,50,52,54,56,58,60,62,0,2,4,6,8,10,12,14,16,..., dimensions={0} | all-to-all | bytes 32768 | tf_op jit(solution)/shard_map/all_to_all | solution.py:429
  58.7 1.1 %finish.1 = (f32[32,3,128]{2,1,0:T(4,128)}, f32[32,3,128]{2,1,0:T(4,128)}) custom-call(f32[15,32,128]{2,1,0:T(8,128)S(1)} %get-tuple-element.12.basis_ref, f32[4,8,128]{2,1,0:T(8,128)S(1)} %bitcast.20), custom_call_target="tpu_custom_call" | custom-call | tf_op jit(solution)/shard_map/finish/pallas_call | solution.py:438
  (2 shorter events, 0.0 us)
Async XLA Ops:
  1.8 31.4 %collective-permute-start.2 = (f32[10,32,128]{2,1,0:T(8,128)S(1)}, f32[10,32,128]{2,1,0:T(8,128)S(1)}, u32[]{:S(2)}, u32[]{:S(2)}) collective-permute-start(f32[10,32,128]{2,1,0:T(8,128)S(1)} %get-tuple-element.10.own_ref), channel_id=1, source_target_pairs={{0,63},{1,0},{2,1},{3,2},{4,3},{5,4},{6,5},{7,6},{8,7},{9,8},{10,9... | collective-permute-start | bytes 491528 | tf_op jit(solution)/shard_map/ppermute | solution.py:407
  22.3 10.9 %collective-permute-start.1 = (f32[10,32,128]{2,1,0:T(8,128)S(1)}, f32[10,32,128]{2,1,0:T(8,128)S(1)}, u32[]{:S(2)}, u32[]{:S(2)}) collective-permute-start(f32[10,32,128]{2,1,0:T(8,128)S(1)} %get-tuple-element.10.own_ref), channel_id=1, source_target_pairs={{0,1},{1,2},{2,3},{3,4},{4,5},{5,6},{6,7},{7,8},{8,9},{9,10},{10,1... | collective-permute-start | bytes 491528 | tf_op jit(solution)/shard_map/ppermute | solution.py:407
  22.3 10.9 %collective-permute-start = (f32[12,16,128]{2,1,0:T(8,128)S(1)}, f32[12,16,128]{2,1,0:T(8,128)S(1)}, u32[]{:S(2)}, u32[]{:S(2)}) collective-permute-start(f32[12,16,128]{2,1,0:T(8,128)S(1)} %get-tuple-element.9), channel_id=1, source_target_pairs={{0,2},{1,3},{2,4},{3,5},{4,6},{5,7},{6,8},{7,9},{8,10},{9,11},{10,... | collective-permute-start | bytes 294920 | tf_op jit(solution)/shard_map/ppermute | solution.py:407
  22.3 7.6 %collective-permute-start.3 = (f32[10,16,128]{2,1,0:T(8,128)S(1)}, f32[10,16,128]{2,1,0:T(8,128)S(1)}, u32[]{:S(2)}, u32[]{:S(2)}) collective-permute-start(f32[10,16,128]{2,1,0:T(8,128)S(1)} %get-tuple-element.11), channel_id=1, source_target_pairs={{0,62},{1,63},{2,0},{3,1},{4,2},{5,3},{6,4},{7,5},{8,6},{9,7},{10,... | collective-permute-start | bytes 245768 | tf_op jit(solution)/shard_map/ppermute | solution.py:407
  34.4 1.2 %collective-permute-start.4 = (f32[1,128]{1,0:T(1,128)S(1)}, f32[1,128]{1,0:T(1,128)S(1)}, u32[]{:S(2)}, u32[]{:S(2)}) collective-permute-start(f32[1,128]{1,0:T(1,128)S(1)} %get-tuple-element.13), channel_id=1, source_target_pairs={{0,1},{1,0},{2,3},{3,2},{4,5},{5,4},{6,7},{7,6},{8,9},{9,8},{10,11... | collective-permute-start | bytes 1544 | tf_op jit(solution)/shard_map/ppermute | solution.py:407
